TPU v7x, 256 devices: a whole 4x4x8 slice. The times are simulated.
256 devices in a mesh: layer: 16 (over z_hi, x), rep: 16 (over z_lo, y, core).
Axes of the slice: x: 4, y: 4, z: 8 (z_hi: 4, z_lo: 2; z = z_hi * 2 + z_lo), core: 2. Of those that a mesh axis runs over, the one named last changes fastest.
Arguments:
- inverse_root: bfloat16 [128, 16, 128, 128], P('layer', 'rep'), may hold values from -0.625 to 0.625
- square_root: bfloat16 [128, 16, 128, 128], P('layer', 'rep'), may hold values from -0.625 to 0.625
- pattern: int32 [128, 16], P('layer', 'rep'), may hold values from 0 to 1, as said below
Outputs:
- inverse_next: bfloat16 [128, 16, 128, 128], P('layer', 'rep')
- square_next: bfloat16 [128, 16, 128, 128], P('layer', 'rep')
Inputs may be any that keep to these rules, and one draw needn't show every extreme that they name: 1 marks a tile of the common pattern. Slot 8 is 1 in every block row, and slot w of block row i is 0 where i - 8 + w lies outside 0 to 127.
All inputs are finite; a program needn't handle non-finite values.
Results may differ from a plain program's by a relative error of at most 0.018.
Values may be sent and summed in bfloat16 or wider, within the bound.
A program may use at most 64 MiB of HBM per device.

v0:
```python
import jax
import jax.numpy as jnp
from jax import lax
from jax.sharding import Mesh
from jax.sharding import PartitionSpec as P

REP = ("rep_0", "rep_1", "rep_2")


def passed_along(block, axis, distance):
    devices = range(lax.axis_size(axis))
    route = [(i - distance, i) for i in devices if i - distance in devices]
    return lax.ppermute(block, axis, route)


def in_blocks(value, dim, peers):
    before, after = (value.shape[:dim], value.shape[dim + 1 :])
    return jnp.moveaxis(value.reshape(*before, peers, -1, *after), dim, 0)


def sum_at_owner(value, axis, dim):
    peers = lax.axis_size(axis)
    parts = lax.all_to_all(in_blocks(value, dim, peers), axis, 0, 0, tiled=True)
    return jnp.sum(parts.astype(jnp.float32), axis=0)


def sum_by_axis(value, axes, dim):
    far, near = axes
    parts = in_blocks(value, dim, lax.axis_size(far))
    nearer = sum_at_owner(parts, near, dim + 1)
    arrived = lax.all_to_all(
        nearer.astype(jnp.bfloat16), far, split_axis=0, concat_axis=0, tiled=True
    )
    return arrived.astype(jnp.float32).sum(axis=0)


def band_product(left_tiles, right_tiles):
    row_count = left_tiles.shape[0]
    slot_count = left_tiles.shape[1]
    groups = lax.axis_size(REP)
    band_slots = slot_count * groups
    half_band = band_slots // 2
    window_rows = row_count + slot_count - 1
    depth_rows = -(-half_band // row_count)
    offsets = list(range(depth_rows, 0, -1)) + list(range(-1, -depth_rows - 1, -1))
    shifted = [passed_along(right_tiles, "layer", shift_by) for shift_by in offsets]
    extended = jnp.concatenate(shifted[:depth_rows] + [right_tiles] + shifted[depth_rows:], axis=0)
    first_row = depth_rows * row_count - half_band
    row_index = (
        first_row
        + jnp.arange(groups, dtype=jnp.int32)[:, None] * slot_count
        + jnp.arange(window_rows, dtype=jnp.int32)[None, :]
    )
    outgoing = jnp.take(extended, row_index, axis=0)
    incoming = lax.all_to_all(outgoing, REP, split_axis=0, concat_axis=2, tiled=True)[0]
    replica = lax.axis_index(REP)
    product = jnp.einsum(
        "iab,ivbc->ivac", left_tiles[:, 0], incoming, preferred_element_type=jnp.float32
    )
    padded = jnp.pad(product, ((0, 0), (band_slots, band_slots), (0, 0), (0, 0)))
    offset = band_slots + half_band - replica * slot_count
    partial_value = lax.dynamic_slice_in_dim(padded, offset, band_slots, axis=1)
    return sum_by_axis(partial_value.astype(jnp.bfloat16), (("rep_0", "rep_1"), "rep_2"), 1)


def body(inverse_root, square_root, pattern):
    in_pattern = (pattern == 1)[:, :, None, None]
    inverse_kept = jnp.where(in_pattern, inverse_root, jnp.zeros_like(inverse_root))
    square_kept = jnp.where(in_pattern, square_root, jnp.zeros_like(square_root))
    intersection = jnp.where(in_pattern, band_product(inverse_kept, square_kept), jnp.float32(0.0))
    slot_count = pattern.shape[1]
    half_band = slot_count * lax.axis_size(REP) // 2
    slot_ids = lax.axis_index(REP) * slot_count + jnp.arange(slot_count, dtype=jnp.int32)
    diagonal = (slot_ids == half_band).astype(jnp.float32)
    identity = jnp.eye(inverse_root.shape[2], dtype=jnp.float32)
    update = jnp.where(
        in_pattern,
        1.5 * diagonal[None, :, None, None] * identity - 0.5 * intersection,
        jnp.float32(0.0),
    ).astype(jnp.bfloat16)
    square_next = jnp.where(in_pattern, band_product(square_kept, update), jnp.float32(0.0)).astype(
        jnp.bfloat16
    )
    inverse_next = jnp.where(
        in_pattern, band_product(update, inverse_kept), jnp.float32(0.0)
    ).astype(jnp.bfloat16)
    return (inverse_next, square_next)


def solution(mesh):
    torus = Mesh(
        mesh.devices.reshape(mesh.shape["layer"], 2, 4, 2), ("layer", "rep_0", "rep_1", "rep_2")
    )
    return jax.shard_map(
        body,
        mesh=torus,
        in_specs=(P("layer", REP, None, None), P("layer", REP, None, None), P("layer", REP)),
        out_specs=(P("layer", REP, None, None), P("layer", REP, None, None)),
        check_vma=False,
    )
```

profile of v0, /device:TPU:71, one launch (start us, length us, event | category | flops | bytes accessed | tf_op | source)
XLA Modules:
  0.0 432.4 jit_solution(6950178988389279599)
XLA Ops:
  0.6 0.7 compare_bitcast_fusion
  1.3 1.1 broadcast_select_fusion.3
  2.4 2.5 collective-permute-start.3
  4.9 7.0 %collective-permute-start.2 = (bf16[8,1,128,128]{3,2,1,0:T(8,128)(2,1)S(1)}, bf16[8,1,128,128]{3,2,1,0:T(8,128)(2,1)S(1)}, u32[]{:S(2)}, u32[]{:S(2)}) collective-permute-start(bf16[8,1,128,128]{3,2,1,0:T(8,128)(2,1)S(1)} %get-tuple-element.7), channel_id=1, source_target_pairs={{0,16},{16,32},{32,48},{48,64},{64,80},{80,96},{96,112},{112,128},... | collective-permute-start | bytes 786440 | tf_op jit(solution)/shard_map/ppermute | solution.py:13
  12.0 0.1 reshape.166
  12.1 9.3 %collective-permute-done.3 = bf16[8,1,128,128]{3,2,1,0:T(8,128)(2,1)S(1)} collective-permute-done((bf16[8,1,128,128]{3,2,1,0:T(8,128)(2,1)S(1)}, bf16[8,1,128,128]{3,2,1,0:T(8,128)(2,1)S(1)}, u32[]{:S(2)}, u32[]{:S(2)}) %collective-permute-start.3) | collective-permute-done | bytes 262176 | tf_op jit(solution)/shard_map/ppermute | solution.py:13
  21.3 0.7 collective-permute-done.2
  22.1 0.1 maximum_bitcast_fusion.1
  22.1 3.1 gather_fusion.1
  25.2 4.6 %broadcast_select_fusion.1 = bf16[16,8,1,128,128]{4,3,1,0,2:T(8,128)(2,1)} fusion(bf16[16,8,1,128,128]{4,3,1,0,2:T(8,128)(2,1)} %bitcast.110, pred[16,8]{1,0:T(8,128)(4,1)S(1)} %compare_and_fusion), kind=kLoop, calls=%fused_computation.25 | loop fusion | flops 2097152 | bytes 8388736 | tf_op jit(solution)/shard_map/jit(_take)/select_n | solution.py:54
  29.8 6.4 %copy.16 = bf16[16,8,1,128,128]{3,4,1,2,0:T(8,128)(2,1)} copy(bf16[16,8,1,128,128]{4,3,1,0,2:T(8,128)(2,1)} %broadcast_select_fusion.1) | data formatting | bytes 8388608 | tf_op jit(solution)/shard_map/jit(_take)/select_n | solution.py:54
  36.2 6.5 %all-to-all-start.1 = ((bf16[16,8,1,128,128]{3,4,1,2,0:T(8,128)(2,1)}), bf16[16,8,1,128,128]{3,4,1,2,0:T(8,128)(2,1)}, u32[]{:S(2)}, u32[]{:S(2)}) async-start(bf16[16,8,1,128,128]{3,4,1,2,0:T(8,128)(2,1)} %copy.16), calls=%async_computation.1 | async-start | bytes 8388608 | tf_op jit(solution)/shard_map/all_to_all | solution.py:55
  42.7 56.2 %all-to-all-done.1 = bf16[16,8,1,128,128]{3,4,1,2,0:T(8,128)(2,1)} async-done(((bf16[16,8,1,128,128]{3,4,1,2,0:T(8,128)(2,1)}), bf16[16,8,1,128,128]{3,4,1,2,0:T(8,128)(2,1)}, u32[]{:S(2)}, u32[]{:S(2)}) %all-to-all-start.1) | async-done | bytes 4194336 | tf_op jit(solution)/shard_map/all_to_all | solution.py:55
  98.9 3.4 fusion.15
  102.4 1.5 fusion
  103.9 0.3 copy.58
  104.2 8.5 %all_to_all.75 = bf16[2,8,8,1,128,128]{4,5,1,2,3,0:T(8,128)(2,1)} all-to-all(bf16[2,8,8,1,128,128]{4,5,1,2,3,0:T(8,128)(2,1)S(1)} %bitcast.113), channel_id=1, replica_groups=mesh['layer'=16,'rep_0'=2,'rep_1'=4,'rep_2'=2] {'rep_2'}, dimensions={0} | all-to-all | bytes 8388608 | tf_op jit(solution)/shard_map/all_to_all | solution.py:23
  112.7 3.5 reduce_sum.75
  116.2 2.6 copy.20
  118.8 10.3 %all-to-all-start.3 = ((bf16[8,8,1,128,128]{4,3,1,2,0:T(8,128)(2,1)}), bf16[8,8,1,128,128]{4,3,1,2,0:T(8,128)(2,1)S(1)}, u32[]{:S(2)}, u32[]{:S(2)}) async-start(bf16[8,8,1,128,128]{4,3,1,2,0:T(8,128)(2,1)} %copy.20), calls=%async_computation.3 | async-start | bytes 4194304 | tf_op jit(solution)/shard_map/all_to_all | solution.py:31
  129.1 1.9 collective-permute-start.1
  131.0 8.4 %collective-permute-start = (bf16[8,1,128,128]{3,2,1,0:T(8,128)(2,1)S(1)}, bf16[8,1,128,128]{3,2,1,0:T(8,128)(2,1)}, u32[]{:S(2)}, u32[]{:S(2)}) collective-permute-start(bf16[8,1,128,128]{3,2,1,0:T(8,128)(2,1)S(1)} %get-tuple-element.8), channel_id=1, source_target_pairs={{0,16},{16,32},{32,48},{48,64},{64,80},{80,96},{96,112},{112,128},... | collective-permute-start | bytes 786440 | tf_op jit(solution)/shard_map/ppermute | solution.py:13
  139.4 17.9 %all-to-all-done.3 = bf16[8,8,1,128,128]{4,3,1,2,0:T(8,128)(2,1)S(1)} async-done(((bf16[8,8,1,128,128]{4,3,1,2,0:T(8,128)(2,1)}), bf16[8,8,1,128,128]{4,3,1,2,0:T(8,128)(2,1)S(1)}, u32[]{:S(2)}, u32[]{:S(2)}) %all-to-all-start.3) | async-done | bytes 2097184 | tf_op jit(solution)/shard_map/all_to_all | solution.py:31
  157.3 0.3 convert_reduce_fusion.2
  157.6 0.2 fusion.25
  157.8 1.9 collective-permute-start.5
  159.7 10.9 %collective-permute-start.4 = (bf16[8,1,128,128]{3,2,1,0:T(8,128)(2,1)S(1)}, bf16[8,1,128,128]{3,2,1,0:T(8,128)(2,1)S(1)}, u32[]{:S(2)}, u32[]{:S(2)}) collective-permute-start(bf16[8,1,128,128]{3,2,1,0:T(8,128)(2,1)S(1)} %fusion.25), channel_id=1, source_target_pairs={{0,16},{16,32},{32,48},{48,64},{64,80},{80,96},{96,112},{112,128},... | collective-permute-start | bytes 786440 | tf_op jit(solution)/shard_map/ppermute | solution.py:13
  170.6 0.0 collective-permute-done.1
  170.6 0.0 collective-permute-done
  170.6 1.0 maximum_bitcast_fusion
  171.7 3.0 gather_fusion
  174.7 10.4 %collective-permute-done.5 = bf16[8,1,128,128]{3,2,1,0:T(8,128)(2,1)S(1)} collective-permute-done((bf16[8,1,128,128]{3,2,1,0:T(8,128)(2,1)S(1)}, bf16[8,1,128,128]{3,2,1,0:T(8,128)(2,1)S(1)}, u32[]{:S(2)}, u32[]{:S(2)}) %collective-permute-start.5) | collective-permute-done | bytes 262176 | tf_op jit(solution)/shard_map/ppermute | solution.py:13
  185.1 0.0 collective-permute-done.4
  185.1 0.1 maximum_bitcast_fusion.2
  185.2 3.0 gather_fusion.2
  188.2 5.9 %broadcast_select_fusion = (bf16[16,8,1,128,128]{4,3,1,0,2:T(8,128)(2,1)}, bf16[16,8,1,128,128]{4,3,1,0,2:T(8,128)(2,1)}) fusion(bf16[16,8,1,128,128]{4,3,1,0,2:T(8,128)(2,1)} %bitcast.107, pred[16,8]{1,0:T(8,128)(4,1)S(1)} %compare_and_fusion, bf16[16,8,1,128,128]{4,3,1,0,2:T(8,128)(2,1)} %bitcast.106), kind=kLoop, calls=%fused_computation.24 | loop fusion | flops 4194304 | bytes 16777344 | tf_op jit(solution)/shard_map/jit(_take)/select_n | solution.py:54
  194.1 6.4 %copy.24 = bf16[16,8,1,128,128]{3,4,1,2,0:T(8,128)(2,1)} copy(bf16[16,8,1,128,128]{4,3,1,0,2:T(8,128)(2,1)} %get-tuple-element.3) | data formatting | bytes 8388608 | tf_op jit(solution)/shard_map/jit(_take)/select_n | solution.py:54
  200.5 5.0 %all-to-all-start.6 = ((bf16[16,8,1,128,128]{3,4,1,2,0:T(8,128)(2,1)}), bf16[16,8,1,128,128]{3,4,1,2,0:T(8,128)(2,1)}, u32[]{:S(2)}, u32[]{:S(2)}) async-start(bf16[16,8,1,128,128]{3,4,1,2,0:T(8,128)(2,1)} %copy.24), calls=%async_computation.6 | async-start | bytes 8388608 | tf_op jit(solution)/shard_map/all_to_all | solution.py:55
  205.5 6.4 %copy.14 = bf16[16,8,1,128,128]{3,4,1,2,0:T(8,128)(2,1)} copy(bf16[16,8,1,128,128]{4,3,1,0,2:T(8,128)(2,1)} %get-tuple-element.4) | data formatting | bytes 8388608 | tf_op jit(solution)/shard_map/jit(_take)/select_n | solution.py:54
  211.9 48.8 %all-to-all-done.6 = bf16[16,8,1,128,128]{3,4,1,2,0:T(8,128)(2,1)} async-done(((bf16[16,8,1,128,128]{3,4,1,2,0:T(8,128)(2,1)}), bf16[16,8,1,128,128]{3,4,1,2,0:T(8,128)(2,1)}, u32[]{:S(2)}, u32[]{:S(2)}) %all-to-all-start.6) | async-done | bytes 4194336 | tf_op jit(solution)/shard_map/all_to_all | solution.py:55
  260.7 11.5 %all-to-all-start = ((bf16[16,8,1,128,128]{3,4,1,2,0:T(8,128)(2,1)}), bf16[16,8,1,128,128]{3,4,1,2,0:T(8,128)(2,1)}, u32[]{:S(2)}, u32[]{:S(2)}) async-start(bf16[16,8,1,128,128]{3,4,1,2,0:T(8,128)(2,1)} %copy.14), calls=%async_computation | async-start | bytes 8388608 | tf_op jit(solution)/shard_map/all_to_all | solution.py:55
  272.1 5.4 %fusion.18 = bf16[8,16,128,128]{2,3,1,0:T(8,128)(2,1)} fusion(bf16[16,8,1,128,128]{3,4,1,2,0:T(8,128)(2,1)} %all-to-all-done.6, bf16[8,1,128,128]{3,2,1,0:T(8,128)(2,1)S(1)} %get-tuple-element.7), kind=kOutput, calls=%fused_computation.29 | convolution fusion | flops 536870912 | bytes 8650752 | tf_op jit(solution)/shard_map/iab,ivbc->ivac/dot_general | solution.py:57
  277.5 50.8 %all-to-all-done = bf16[16,8,1,128,128]{3,4,1,2,0:T(8,128)(2,1)} async-done(((bf16[16,8,1,128,128]{3,4,1,2,0:T(8,128)(2,1)}), bf16[16,8,1,128,128]{3,4,1,2,0:T(8,128)(2,1)}, u32[]{:S(2)}, u32[]{:S(2)}) %all-to-all-start) | async-done | bytes 4194336 | tf_op jit(solution)/shard_map/all_to_all | solution.py:55
  328.3 0.0 copy-start
  328.3 3.7 fusion.12
  332.0 0.0 copy-done
  332.0 3.1 fusion.1
  335.1 2.2 copy.57
  337.4 0.6 copy.56
  337.9 8.4 %all_to_all.76 = bf16[2,8,8,1,128,128]{4,5,1,2,3,0:T(8,128)(2,1)} all-to-all(bf16[2,8,8,1,128,128]{4,5,1,2,3,0:T(8,128)(2,1)S(1)} %bitcast.114), channel_id=1, replica_groups=mesh['layer'=16,'rep_0'=2,'rep_1'=4,'rep_2'=2] {'rep_2'}, dimensions={0} | all-to-all | bytes 8388608 | tf_op jit(solution)/shard_map/all_to_all | solution.py:23
  346.3 3.5 reduce_sum.83
  349.8 2.6 copy.28
  352.4 11.9 %all_to_all.77 = bf16[2,8,8,1,128,128]{4,5,1,2,3,0:T(8,128)(2,1)} all-to-all(bf16[2,8,8,1,128,128]{4,5,1,2,3,0:T(8,128)(2,1)} %bitcast.111), channel_id=1, replica_groups=mesh['layer'=16,'rep_0'=2,'rep_1'=4,'rep_2'=2] {'rep_2'}, dimensions={0} | all-to-all | bytes 8388608 | tf_op jit(solution)/shard_map/all_to_all | solution.py:23
  364.3 10.6 %all-to-all-start.8 = ((bf16[8,8,1,128,128]{4,3,1,2,0:T(8,128)(2,1)}), bf16[8,8,1,128,128]{4,3,1,2,0:T(8,128)(2,1)}, u32[]{:S(2)}, u32[]{:S(2)}) async-start(bf16[8,8,1,128,128]{4,3,1,2,0:T(8,128)(2,1)} %copy.28), calls=%async_computation.8 | async-start | bytes 4194304 | tf_op jit(solution)/shard_map/all_to_all | solution.py:31
  374.9 3.5 reduce_sum.78
  378.4 2.6 copy.23
  381.0 20.2 %all-to-all-done.8 = bf16[8,8,1,128,128]{4,3,1,2,0:T(8,128)(2,1)} async-done(((bf16[8,8,1,128,128]{4,3,1,2,0:T(8,128)(2,1)}), bf16[8,8,1,128,128]{4,3,1,2,0:T(8,128)(2,1)}, u32[]{:S(2)}, u32[]{:S(2)}) %all-to-all-start.8) | async-done | bytes 2097184 | tf_op jit(solution)/shard_map/all_to_all | solution.py:31
  401.2 3.7 all-to-all-start.5
  404.8 1.9 convert_reduce_fusion
  406.8 24.3 %all-to-all-done.5 = bf16[8,8,1,128,128]{4,3,1,2,0:T(8,128)(2,1)S(1)} async-done(((bf16[8,8,1,128,128]{4,3,1,2,0:T(8,128)(2,1)}), bf16[8,8,1,128,128]{4,3,1,2,0:T(8,128)(2,1)S(1)}, u32[]{:S(2)}, u32[]{:S(2)}) %all-to-all-start.5) | async-done | bytes 2097184 | tf_op jit(solution)/shard_map/all_to_all | solution.py:31
  431.0 0.3 convert_reduce_fusion.1
  431.4 1.0 fusion.21
  (4 shorter events, 0.0 us)
Async XLA Ops:
  2.4 18.9 %collective-permute-start.3 = (bf16[8,1,128,128]{3,2,1,0:T(8,128)(2,1)S(1)}, bf16[8,1,128,128]{3,2,1,0:T(8,128)(2,1)S(1)}, u32[]{:S(2)}, u32[]{:S(2)}) collective-permute-start(bf16[8,1,128,128]{3,2,1,0:T(8,128)(2,1)S(1)} %get-tuple-element.7), channel_id=1, source_target_pairs={{16,0},{32,16},{48,32},{64,48},{80,64},{96,80},{112,96},{128,112},... | collective-permute-start | bytes 786440 | tf_op jit(solution)/shard_map/ppermute | solution.py:13
  4.9 17.2 %collective-permute-start.2 = (bf16[8,1,128,128]{3,2,1,0:T(8,128)(2,1)S(1)}, bf16[8,1,128,128]{3,2,1,0:T(8,128)(2,1)S(1)}, u32[]{:S(2)}, u32[]{:S(2)}) collective-permute-start(bf16[8,1,128,128]{3,2,1,0:T(8,128)(2,1)S(1)} %get-tuple-element.7), channel_id=1, source_target_pairs={{0,16},{16,32},{32,48},{48,64},{64,80},{80,96},{96,112},{112,128},... | collective-permute-start | bytes 786440 | tf_op jit(solution)/shard_map/ppermute | solution.py:13
  36.2 62.7 %all-to-all-start.1 = ((bf16[16,8,1,128,128]{3,4,1,2,0:T(8,128)(2,1)}), bf16[16,8,1,128,128]{3,4,1,2,0:T(8,128)(2,1)}, u32[]{:S(2)}, u32[]{:S(2)}) async-start(bf16[16,8,1,128,128]{3,4,1,2,0:T(8,128)(2,1)} %copy.16), calls=%async_computation.1 | async-start | bytes 8388608 | tf_op jit(solution)/shard_map/all_to_all | solution.py:55
  118.8 38.5 %all-to-all-start.3 = ((bf16[8,8,1,128,128]{4,3,1,2,0:T(8,128)(2,1)}), bf16[8,8,1,128,128]{4,3,1,2,0:T(8,128)(2,1)S(1)}, u32[]{:S(2)}, u32[]{:S(2)}) async-start(bf16[8,8,1,128,128]{4,3,1,2,0:T(8,128)(2,1)} %copy.20), calls=%async_computation.3 | async-start | bytes 4194304 | tf_op jit(solution)/shard_map/all_to_all | solution.py:31
  129.1 41.5 %collective-permute-start.1 = (bf16[8,1,128,128]{3,2,1,0:T(8,128)(2,1)S(1)}, bf16[8,1,128,128]{3,2,1,0:T(8,128)(2,1)S(1)}, u32[]{:S(2)}, u32[]{:S(2)}) collective-permute-start(bf16[8,1,128,128]{3,2,1,0:T(8,128)(2,1)S(1)} %get-tuple-element.8), channel_id=1, source_target_pairs={{16,0},{32,16},{48,32},{64,48},{80,64},{96,80},{112,96},{128,112},... | collective-permute-start | bytes 786440 | tf_op jit(solution)/shard_map/ppermute | solution.py:13
  131.0 39.6 %collective-permute-start = (bf16[8,1,128,128]{3,2,1,0:T(8,128)(2,1)S(1)}, bf16[8,1,128,128]{3,2,1,0:T(8,128)(2,1)}, u32[]{:S(2)}, u32[]{:S(2)}) collective-permute-start(bf16[8,1,128,128]{3,2,1,0:T(8,128)(2,1)S(1)} %get-tuple-element.8), channel_id=1, source_target_pairs={{0,16},{16,32},{32,48},{48,64},{64,80},{80,96},{96,112},{112,128},... | collective-permute-start | bytes 786440 | tf_op jit(solution)/shard_map/ppermute | solution.py:13
  157.8 27.3 %collective-permute-start.5 = (bf16[8,1,128,128]{3,2,1,0:T(8,128)(2,1)S(1)}, bf16[8,1,128,128]{3,2,1,0:T(8,128)(2,1)S(1)}, u32[]{:S(2)}, u32[]{:S(2)}) collective-permute-start(bf16[8,1,128,128]{3,2,1,0:T(8,128)(2,1)S(1)} %fusion.25), channel_id=1, source_target_pairs={{16,0},{32,16},{48,32},{64,48},{80,64},{96,80},{112,96},{128,112},... | collective-permute-start | bytes 786440 | tf_op jit(solution)/shard_map/ppermute | solution.py:13
  159.7 25.4 %collective-permute-start.4 = (bf16[8,1,128,128]{3,2,1,0:T(8,128)(2,1)S(1)}, bf16[8,1,128,128]{3,2,1,0:T(8,128)(2,1)S(1)}, u32[]{:S(2)}, u32[]{:S(2)}) collective-permute-start(bf16[8,1,128,128]{3,2,1,0:T(8,128)(2,1)S(1)} %fusion.25), channel_id=1, source_target_pairs={{0,16},{16,32},{32,48},{48,64},{64,80},{80,96},{96,112},{112,128},... | collective-permute-start | bytes 786440 | tf_op jit(solution)/shard_map/ppermute | solution.py:13
  200.5 60.2 %all-to-all-start.6 = ((bf16[16,8,1,128,128]{3,4,1,2,0:T(8,128)(2,1)}), bf16[16,8,1,128,128]{3,4,1,2,0:T(8,128)(2,1)}, u32[]{:S(2)}, u32[]{:S(2)}) async-start(bf16[16,8,1,128,128]{3,4,1,2,0:T(8,128)(2,1)} %copy.24), calls=%async_computation.6 | async-start | bytes 8388608 | tf_op jit(solution)/shard_map/all_to_all | solution.py:55
  260.7 67.6 %all-to-all-start = ((bf16[16,8,1,128,128]{3,4,1,2,0:T(8,128)(2,1)}), bf16[16,8,1,128,128]{3,4,1,2,0:T(8,128)(2,1)}, u32[]{:S(2)}, u32[]{:S(2)}) async-start(bf16[16,8,1,128,128]{3,4,1,2,0:T(8,128)(2,1)} %copy.14), calls=%async_computation | async-start | bytes 8388608 | tf_op jit(solution)/shard_map/all_to_all | solution.py:55
  328.3 3.7 copy-start
  364.3 36.9 %all-to-all-start.8 = ((bf16[8,8,1,128,128]{4,3,1,2,0:T(8,128)(2,1)}), bf16[8,8,1,128,128]{4,3,1,2,0:T(8,128)(2,1)}, u32[]{:S(2)}, u32[]{:S(2)}) async-start(bf16[8,8,1,128,128]{4,3,1,2,0:T(8,128)(2,1)} %copy.28), calls=%async_computation.8 | async-start | bytes 4194304 | tf_op jit(solution)/shard_map/all_to_all | solution.py:31
  401.2 29.9 %all-to-all-start.5 = ((bf16[8,8,1,128,128]{4,3,1,2,0:T(8,128)(2,1)}), bf16[8,8,1,128,128]{4,3,1,2,0:T(8,128)(2,1)S(1)}, u32[]{:S(2)}, u32[]{:S(2)}) async-start(bf16[8,8,1,128,128]{4,3,1,2,0:T(8,128)(2,1)} %copy.23), calls=%async_computation.5 | async-start | bytes 4194304 | tf_op jit(solution)/shard_map/all_to_all | solution.py:31
where the time goes:
time: 434 us; the launch traced here: 432 us
  waiting for transfers between devices  239 us (55%)
  starting transfers between devices  80 us (18%)
  local copies, waits for them, and re-layouts  44.1 us (10%)
  blocking collectives  28.7 us (7%)
  other arithmetic  27.7 us (6%)
  matrix products  12.5 us (3%)
    all_to_all x3, waiting for transfers between devices, band_product(): lax.all_to_all(outgoing, REP, split_axis=0, concat_axis=2, tiled=True)[0]  156 us
    all_to_all x3, waiting for transfers between devices, sum_by_axis(): lax.all_to_all(nearer.astype(jnp.bfloat16), far, split_axis=0, concat_axi...  62.3 us
    ppermute x6, starting transfers between devices, passed_along(): return lax.ppermute(block, axis, route)  32.6 us
    all_to_all x3, blocking collectives, sum_at_owner(): parts = lax.all_to_all(in_blocks(value, dim, peers), axis, 0, 0, tiled=True)  28.7 us
    all_to_all x3, starting transfers between devices, sum_by_axis(): lax.all_to_all(nearer.astype(jnp.bfloat16), far, split_axis=0, concat_axi...  24.5 us
    all_to_all x3, starting transfers between devices, band_product(): lax.all_to_all(outgoing, REP, split_axis=0, concat_axis=2, tiled=True)[0]  22.9 us
    ppermute x6, waiting for transfers between devices, passed_along(): return lax.ppermute(block, axis, route)  20.4 us
    select_n x3, local copies, waits for them, and re-layouts, band_product(): outgoing = jnp.take(extended, row_index, axis=0)  19.2 us
  transfers between devices with their start and end apart: 12, of which 9 were waited for; matrix products, arithmetic and copies ran while one was open for 6% of the time, Pallas kernels for 0%

commit v1 on v0

v1 whole, which is shorter than its diff:
```python
import functools

import jax
import jax.numpy as jnp
from jax import lax
from jax.experimental import pallas as pl
from jax.experimental.pallas import tpu as pltpu
from jax.sharding import PartitionSpec as P

BF = jnp.bfloat16
F32 = jnp.float32
MESH = pl.DeviceIdType.MESH
Z, Y, U = 0, 1, 2


def mod(a, b):
    return lax.rem(a, jnp.int32(b))


def div(a, b):
    return lax.div(a, jnp.int32(b))


def kernel(
    layers, t,
    z_hbm, y_hbm, pat_ref, w_out, x_out,
    raw, kept, marks, marks_home, left, right, lhs, rhs, prod, give, got, done, land,
    in_sem, home_send, home_recv, mark_send, mark_recv,
    left_send, left_recv, right_send, right_recv, pair_send, pair_recv, out_send, out_recv,
):
    l = lax.axis_index("layer")
    r = lax.axis_index("rep")
    h, y, c = div(r, 8), mod(div(r, 2), 4), mod(r, 2)
    big = 2 * l + h
    shift = 8 * mod(l + 1, 2)
    delta = mod(y + 4 * layers * 2 - big, 4)
    other = 1 - c
    pending = []

    def rep_of(hh, yy, cc):
        return hh * 8 + yy * 2 + cc

    def remote(src, dst, send_sem, recv_sem, layer, rep, cond=None):
        copy = pltpu.make_async_remote_copy(
            src_ref=src, dst_ref=dst, send_sem=send_sem, recv_sem=recv_sem,
            device_id=(layer, rep), device_id_type=MESH,
        )
        if cond is None:
            copy.start()
        else:
            pl.when(cond)(copy.start)
        pending.append((cond, copy))

    def arrive(dst, recv_sem, cond=None):
        copy = pltpu.make_async_remote_copy(
            src_ref=dst, dst_ref=dst, send_sem=recv_sem, recv_sem=recv_sem,
            device_id=(l, r), device_id_type=MESH,
        )
        if cond is None:
            copy.wait_recv()
        else:
            pl.when(cond)(copy.wait_recv)

    loads = [
        pltpu.make_async_copy(ref.at[:, 0], raw.at[k], in_sem.at[k])
        for k, ref in ((Z, z_hbm), (Y, y_hbm))
    ]
    for load in loads:
        load.start()

    barrier = pltpu.get_barrier_semaphore()
    for step in range(1, 16):
        pl.semaphore_signal(
            barrier, inc=1, device_id=(l, mod(r + step, 16)), device_id_type=MESH
        )
    for near in (mod(l + 1, layers), mod(l + layers - 1, layers)):
        for hh in range(2):
            for cc in range(2):
                pl.semaphore_signal(
                    barrier, inc=1, device_id=(near, rep_of(hh, y, cc)), device_id_type=MESH
                )

    for ap in range(8):
        marks[ap] = jnp.full((8, 128), pat_ref[ap, 0], jnp.int32)
    for k in (Z, Y):
        loads[k].wait()
        for ap in range(8):
            kept[k, ap] = jnp.where(pat_ref[ap, 0] == 1, raw[k, ap], jnp.zeros((t, t), BF))
    pl.semaphore_wait(barrier, 23)

    def scatter(k):
        for ap in range(8):
            jm = mod(shift + ap + r, 16)
            yd, cd, b2 = div(jm, 4), div(mod(jm, 4), 2), mod(jm, 2)
            dest = rep_of(ap // 4, yd, cd)
            here, away = dest == r, dest != r
            a = ap % 4

            @pl.when(here)
            def _():
                left[k, yd, a, b2] = kept[k, ap]
                if k == Y:
                    marks_home[a, b2] = marks[ap]

            remote(
                kept.at[k, ap], left.at[k, yd, a, b2], home_send.at[k, ap],
                home_recv.at[k, a, b2], l, dest, away,
            )
            if k == Y:
                remote(
                    marks.at[ap], marks_home.at[a, b2], mark_send.at[ap],
                    mark_recv.at[a, b2], l, dest, away,
                )

    def from_other(a, b2):
        source = mod(4 * y + 2 * c + b2 - shift - (4 * h + a) + 32, 16)
        return source != r

    def home_ready(k):
        for a in range(4):
            for b2 in range(2):
                arrive(left.at[k, y, a, b2], home_recv.at[k, a, b2], from_other(a, b2))

    up, down = mod(y + 1, 4), mod(y + 3, 4)
    far = mod(y + 2, 4)

    def left_start(k):
        for step, half in ((0, 0), (1, 1)):
            part = pl.ds(2 * half, 2)
            remote(
                left.at[k, y, part], left.at[k, y, part], left_send.at[k, half],
                left_recv.at[k, half], l, rep_of(h, up, c),
            )
            back = 1 - half
            part = pl.ds(2 * back, 2)
            remote(
                left.at[k, y, part], left.at[k, y, part], left_send.at[k, 2 + back],
                left_recv.at[k, 2 + back], l, rep_of(h, down, c),
            )

    def left_forward(k):
        arrive(left.at[k, down, pl.ds(0, 2)], left_recv.at[k, 0])
        remote(
            left.at[k, down, pl.ds(0, 2)], left.at[k, down, pl.ds(0, 2)], left_send.at[k, 4],
            left_recv.at[k, 4], l, rep_of(h, up, c),
        )
        arrive(left.at[k, up, pl.ds(2, 2)], left_recv.at[k, 3])
        remote(
            left.at[k, up, pl.ds(2, 2)], left.at[k, up, pl.ds(2, 2)], left_send.at[k, 5],
            left_recv.at[k, 5], l, rep_of(h, down, c),
        )

    def left_ready(k):
        arrive(left.at[k, down, pl.ds(2, 2)], left_recv.at[k, 1])
        arrive(left.at[k, up, pl.ds(0, 2)], left_recv.at[k, 2])
        arrive(left.at[k, far, pl.ds(0, 2)], left_recv.at[k, 4])
        arrive(left.at[k, far, pl.ds(2, 2)], left_recv.at[k, 5])

    def right_start(k):
        for d in (2, -2, 1, -1):
            there = mod(big + d + 2 * layers, 2 * layers)
            ld, hd = div(there, 2), mod(there, 2)
            cond = None
            if d == 2:
                cond = mod(delta + 4 - d, 4) != 1
            if d == -2:
                cond = mod(delta + 4 - d, 4) != 3
            for cd in range(2):
                remote(
                    left.at[k, y, pl.ds(2 * cd, 2)], right.at[k, 2 - d, c],
                    right_send.at[k, 2 - d, cd], right_recv.at[k, 2 - d, c],
                    ld, rep_of(hd, y, cd), cond,
                )
        remote(
            left.at[k, y, pl.ds(2 * other, 2)], right.at[k, 2, c],
            right_send.at[k, 2, 0], right_recv.at[k, 2, c], l, rep_of(h, y, other),
        )
        right[k, 2, c] = left[k, y, pl.ds(2 * c, 2)]

    def right_ready(k):
        arrive(right.at[k, 2, other], right_recv.at[k, 2, other])
        for n in (1, 3, 0, 4):
            cond = None
            if n == 0:
                cond = delta != 1
            if n == 4:
                cond = delta != 3
            for cc in range(2):
                arrive(right.at[k, n, cc], right_recv.at[k, n, cc], cond)

    nothing = jnp.zeros((t, t), BF)
    apart = delta == 2
    toward = jnp.where(delta == 3, -1, delta)
    middle = (jnp.where(apart, -2, toward), jnp.where(apart, 2, toward))

    def multiply(kl, kr):
        for s in range(2):
            for at, n in enumerate((0, 1, 2) if s == 0 else (2, 3, 4)):
                cls = mod(big + n + 2, 4)
                gap = middle[s] - (n - 2)
                for kk in range(2):
                    inner = 2 * c + kk
                    for a in range(4):
                        tile = left[kl, cls, a, kk]
                        if n == 0:
                            tile = jnp.where(inner >= a, tile, nothing)
                        if n == 4:
                            tile = jnp.where(inner < a, tile, nothing)
                        lhs[s, a * t:(a + 1) * t, (2 * at + kk) * t:(2 * at + kk + 1) * t] = tile
                    for b in range(4):
                        whole = jnp.logical_and(gap >= -1, gap <= 1)
                        low = jnp.logical_and(gap == 2, b < inner)
                        high = jnp.logical_and(gap == -2, b >= inner)
                        good = jnp.logical_or(whole, jnp.logical_or(low, high))
                        if s == 1 and n == 2:
                            good = jnp.logical_and(good, apart)
                        tile = jnp.where(good, right[kr, n, b // 2, kk, b % 2], nothing)
                        rhs[s, (2 * at + kk) * t:(2 * at + kk + 1) * t, b * t:(b + 1) * t] = tile
        for s in range(2):
            for half in range(2):
                out = jnp.dot(
                    lhs[s], rhs[s, :, half * 2 * t:(half + 1) * 2 * t], preferred_element_type=F32
                )
                for a in range(4):
                    for b2 in range(2):
                        prod[s, a, 2 * half + b2] = out[a * t:(a + 1) * t, b2 * t:(b2 + 1) * t]

    def total(a, b):
        first = jnp.logical_or(jnp.logical_not(apart), b >= a)
        second = jnp.logical_or(jnp.logical_not(apart), b < a)
        empty = jnp.zeros((t, t), F32)
        return jnp.where(first, prod[0, a, b], empty) + jnp.where(second, prod[1, a, b], empty)

    def share(k):
        for a in range(4):
            for b2 in range(2):
                give[k, a, b2] = total(a, 2 * other + b2).astype(BF)
                prod[0, a, 2 * c + b2] = total(a, 2 * c + b2)
        remote(
            give.at[k], got.at[k], pair_send.at[k], pair_recv.at[k], l, rep_of(h, y, other)
        )

    def summed(k, a, b2):
        value = prod[0, a, 2 * c + b2] + got[k, a, b2].astype(F32)
        return value

    def marked(a, b2):
        return marks_home[a, b2][0:1, :] == 1

    def owner_send(k):
        for a in range(4):
            for b2 in range(2):
                slot = mod(4 * y + 2 * c + b2 + shift - (4 * h + a) + 32, 16)
                done[k, a, b2] = jnp.where(
                    marked(a, b2), summed(k, a, b2), jnp.zeros((t, t), F32)
                ).astype(BF)
        for a in range(4):
            for b2 in range(2):
                slot = mod(4 * y + 2 * c + b2 + shift - (4 * h + a) + 32, 16)
                here, away = slot == r, slot != r

                @pl.when(here)
                def _():
                    land[k, 4 * h + a] = done[k, a, b2]

                remote(
                    done.at[k, a, b2], land.at[k, 4 * h + a], out_send.at[k, a, b2],
                    out_recv.at[k, 4 * h + a], l, slot, away,
                )

    def owner_ready(k, out_ref):
        for ap in range(8):
            jm = mod(shift + ap + r, 16)
            source = rep_of(ap // 4, div(jm, 4), div(mod(jm, 4), 2))
            arrive(land.at[k, ap], out_recv.at[k, ap], source != r)
        for ap in range(8):
            out_ref[ap, 0] = land[k, ap]

    scatter(Y)
    scatter(Z)
    home_ready(Y)
    right_start(Y)
    home_ready(Z)
    left_start(Z)
    right_start(Z)
    left_forward(Z)
    left_start(Y)
    for a in range(4):
        for b2 in range(2):
            arrive(marks_home.at[a, b2], mark_recv.at[a, b2], from_other(a, b2))
    left_ready(Z)
    right_ready(Y)
    multiply(Z, Y)
    share(U)
    left_forward(Y)
    arrive(got.at[U], pair_recv.at[U])
    rows = lax.broadcasted_iota(jnp.int32, (t, t), 0)
    cols = lax.broadcasted_iota(jnp.int32, (t, t), 1)
    for a in range(4):
        for b2 in range(2):
            on = jnp.logical_and(mod(big, 4) == y, 2 * c + b2 == a)
            eye = jnp.where(rows == cols, jnp.where(on, F32(1.5), F32(0.0)), F32(0.0))
            value = eye - 0.5 * summed(U, a, b2)
            left[U, y, a, b2] = jnp.where(marked(a, b2), value, jnp.zeros((t, t), F32)).astype(BF)
    left_start(U)
    right_start(U)
    left_forward(U)
    right_ready(Z)
    left_ready(U)
    multiply(U, Z)
    share(Z)
    arrive(got.at[Z], pair_recv.at[Z])
    owner_send(Z)
    left_ready(Y)
    right_ready(U)
    multiply(Y, U)
    share(Y)
    arrive(got.at[Y], pair_recv.at[Y])
    owner_send(Y)
    owner_ready(Z, w_out)
    owner_ready(Y, x_out)
    for cond, copy in pending:
        if cond is None:
            copy.wait_send()
        else:
            pl.when(cond)(copy.wait_send)


def solution(mesh):
    layers = mesh.shape["layer"]

    def body(inverse_root, square_root, pattern):
        t = inverse_root.shape[-1]
        dma = pltpu.SemaphoreType.DMA
        return pl.pallas_call(
            functools.partial(kernel, layers, t),
            out_shape=[
                jax.ShapeDtypeStruct(inverse_root.shape, BF),
                jax.ShapeDtypeStruct(square_root.shape, BF),
            ],
            in_specs=[
                pl.BlockSpec(memory_space=pl.ANY),
                pl.BlockSpec(memory_space=pl.ANY),
                pl.BlockSpec(memory_space=pltpu.SMEM),
            ],
            out_specs=[pl.BlockSpec(memory_space=pltpu.VMEM)] * 2,
            scratch_shapes=[
                pltpu.VMEM((2, 8, t, t), BF),
                pltpu.VMEM((2, 8, t, t), BF),
                pltpu.VMEM((8, 8, 128), jnp.int32),
                pltpu.VMEM((4, 2, 8, 128), jnp.int32),
                pltpu.VMEM((3, 4, 4, 2, t, t), BF),
                pltpu.VMEM((3, 5, 2, 2, 2, t, t), BF),
                pltpu.VMEM((2, 4 * t, 6 * t), BF),
                pltpu.VMEM((2, 6 * t, 4 * t), BF),
                pltpu.VMEM((2, 4, 4, t, t), F32),
                pltpu.VMEM((3, 4, 2, t, t), BF),
                pltpu.VMEM((3, 4, 2, t, t), BF),
                pltpu.VMEM((2, 4, 2, t, t), BF),
                pltpu.VMEM((2, 8, t, t), BF),
                dma((2,)),
                dma((2, 8)),
                dma((2, 4, 2)),
                dma((8,)),
                dma((4, 2)),
                dma((3, 6)),
                dma((3, 6)),
                dma((3, 5, 2)),
                dma((3, 5, 2)),
                dma((3,)),
                dma((3,)),
                dma((2, 4, 2)),
                dma((2, 8)),
            ],
            compiler_params=pltpu.CompilerParams(
                collective_id=0, has_side_effects=True, vmem_limit_bytes=40 * 1024 * 1024
            ),
            name="band_step",
        )(inverse_root, square_root, pattern)

    return jax.shard_map(
        body,
        mesh=mesh,
        in_specs=(P("layer", "rep", None, None), P("layer", "rep", None, None), P("layer", "rep")),
        out_specs=(P("layer", "rep", None, None), P("layer", "rep", None, None)),
        check_vma=False,
    )
```

time: 434 us -> 104 us (0.24)
  the two profiles are of different devices: /device:TPU:71 before, /device:TPU:1 now
where the time goes in v1:
time: 104 us; the launch traced here: 103 us
  Pallas kernels  98.8 us (95%)
  local copies, waits for them, and re-layouts  4.04 us (4%)
    pallas_call x1, Pallas kernels, body(): pl.pallas_call(functools.partial(kernel, layers, t), out_shape=[jax.Shape...  98.8 us
    unnamed x7, local copies, waits for them, and re-layouts  4.04 us

profile of v1, /device:TPU:1, one launch (start us, length us, event | category | flops | bytes accessed | tf_op | source)
XLA Modules:
  0.0 103.4 jit_solution(2775313292255580669)
XLA Ops:
  0.6 0.7 copy.5.pat_ref
  1.4 0.0 copy-start
  1.4 0.9 copy-done
  2.3 0.0 copy-start.1
  2.3 0.9 copy-done.1
  3.3 98.8 %band_step.1 = (bf16[8,1,128,128]{3,2,1,0:T(8,128)(2,1)S(1)}, bf16[8,1,128,128]{3,2,1,0:T(8,128)(2,1)S(1)}) custom-call(bf16[8,1,128,128]{3,2,1,0:T(8,128)(2,1)S(1)} %copy-done, bf16[8,1,128,128]{3,2,1,0:T(8,128)(2,1)S(1)} %copy-done.1, s32[8,1]{1,0:T(8,128)S(1)} %copy.5.pat_ref), custom_call_target="tpu_custom_call" | custom-call | tf_op jit(solution)/shard_map/band_step/pallas_call | solution.py:335
  102.0 0.7 copy.8
  102.7 0.7 copy.9
Async XLA Ops:
  1.4 0.9 copy-start
  2.3 0.9 copy-start.1

commit v2 on v1

--- a/solution.py
+++ b/solution.py
@@ -26,7 +26,7 @@
     z_hbm, y_hbm, pat_ref, w_out, x_out,
     raw, kept, marks, marks_home, left, right, lhs, rhs, prod, give, got, done, land,
     in_sem, home_send, home_recv, mark_send, mark_recv,
-    left_send, left_recv, right_send, right_recv, pair_send, pair_recv, out_send, out_recv,
+    left_send, left_recv, right_send, right_recv, relay_send, pair_send, pair_recv, out_send, out_recv,
 ):
     l = lax.axis_index("layer")
     r = lax.axis_index("rep")
@@ -73,12 +73,17 @@
         pl.semaphore_signal(
             barrier, inc=1, device_id=(l, mod(r + step, 16)), device_id_type=MESH
         )
-    for near in (mod(l + 1, layers), mod(l + layers - 1, layers)):
-        for hh in range(2):
-            for cc in range(2):
-                pl.semaphore_signal(
-                    barrier, inc=1, device_id=(near, rep_of(hh, y, cc)), device_id_type=MESH
-                )
+    above, below = l < layers - 1, l > 0
+    for near, there in ((l + 1, above), (l - 1, below)):
+
+        @pl.when(there)
+        def _():
+            for hh in range(2):
+                for cc in range(2):
+                    pl.semaphore_signal(
+                        barrier, inc=1, device_id=(near, rep_of(hh, y, cc)), device_id_type=MESH
+                    )
+
 
     for ap in range(8):
         marks[ap] = jnp.full((8, 128), pat_ref[ap, 0], jnp.int32)
@@ -86,7 +91,8 @@
         loads[k].wait()
         for ap in range(8):
             kept[k, ap] = jnp.where(pat_ref[ap, 0] == 1, raw[k, ap], jnp.zeros((t, t), BF))
-    pl.semaphore_wait(barrier, 23)
+    peers = 15 + 4 * (above.astype(jnp.int32) + below.astype(jnp.int32))
+    pl.semaphore_wait(barrier, peers)
 
     def scatter(k):
         for ap in range(8):
@@ -156,15 +162,38 @@
         arrive(left.at[k, far, pl.ds(0, 2)], left_recv.at[k, 4])
         arrive(left.at[k, far, pl.ds(2, 2)], left_recv.at[k, 5])
 
+    first, last = h == 0, h == 1
+    edge_up, edge_down = mod(l, 4) == 3, mod(l, 4) == 0
+    both = jnp.logical_and
+
+    def inside(n):
+        row = big + n - 2
+        return both(row >= 0, row < 2 * layers)
+
+    def wanted(n, dl):
+        if n == 0:
+            return dl != 1
+        if n == 4:
+            return dl != 3
+        return None
+
+    def needed(n):
+        cond = inside(n)
+        want = wanted(n, delta)
+        return cond if want is None else both(cond, want)
+
     def right_start(k):
         for d in (2, -2, 1, -1):
-            there = mod(big + d + 2 * layers, 2 * layers)
+            there = big + d
             ld, hd = div(there, 2), mod(there, 2)
-            cond = None
+            cond = both(there >= 0, there < 2 * layers)
+            want = wanted(2 - d, mod(delta + 4 - d, 4))
+            if want is not None:
+                cond = both(cond, want)
             if d == 2:
-                cond = mod(delta + 4 - d, 4) != 1
+                cond = both(cond, jnp.logical_not(both(last, edge_up)))
             if d == -2:
-                cond = mod(delta + 4 - d, 4) != 3
+                cond = both(cond, jnp.logical_not(both(first, edge_down)))
             for cd in range(2):
                 remote(
                     left.at[k, y, pl.ds(2 * cd, 2)], right.at[k, 2 - d, c],
@@ -177,14 +206,25 @@
         )
         right[k, 2, c] = left[k, y, pl.ds(2 * c, 2)]
 
+    def right_relay(k):
+        for src, dst, side, step in ((1, 0, both(first, both(edge_down, below)), 3),
+                                     (3, 4, both(last, both(edge_up, above)), 1)):
+            for cc in range(2):
+                arrive(right.at[k, src, cc], right_recv.at[k, src, cc], side)
+                remote(
+                    right.at[k, src, cc], right.at[k, dst, cc], relay_send.at[k, cc],
+                    right_recv.at[k, dst, cc], l, rep_of(1 - h, y, c),
+                    both(side, wanted(dst, mod(delta + step, 4))),
+                )
+
     def right_ready(k):
         arrive(right.at[k, 2, other], right_recv.at[k, 2, other])
         for n in (1, 3, 0, 4):
-            cond = None
-            if n == 0:
-                cond = delta != 1
-            if n == 4:
-                cond = delta != 3
+            cond = needed(n)
+            if n == 1:
+                cond = both(cond, jnp.logical_not(both(first, edge_down)))
+            if n == 3:
+                cond = both(cond, jnp.logical_not(both(last, edge_up)))
             for cc in range(2):
                 arrive(right.at[k, n, cc], right_recv.at[k, n, cc], cond)
 
@@ -212,6 +252,8 @@
                         low = jnp.logical_and(gap == 2, b < inner)
                         high = jnp.logical_and(gap == -2, b >= inner)
                         good = jnp.logical_or(whole, jnp.logical_or(low, high))
+                        if n != 2:
+                            good = both(good, inside(n))
                         if s == 1 and n == 2:
                             good = jnp.logical_and(good, apart)
                         tile = jnp.where(good, right[kr, n, b // 2, kk, b % 2], nothing)
@@ -282,8 +324,9 @@
     right_start(Y)
     home_ready(Z)
     left_start(Z)
+    left_forward(Z)
+    right_relay(Y)
     right_start(Z)
-    left_forward(Z)
     left_start(Y)
     for a in range(4):
         for b2 in range(2):
@@ -293,6 +336,7 @@
     multiply(Z, Y)
     share(U)
     left_forward(Y)
+    right_relay(Z)
     arrive(got.at[U], pair_recv.at[U])
     rows = lax.broadcasted_iota(jnp.int32, (t, t), 0)
     cols = lax.broadcasted_iota(jnp.int32, (t, t), 1)
@@ -305,6 +349,7 @@
     left_start(U)
     right_start(U)
     left_forward(U)
+    right_relay(U)
     right_ready(Z)
     left_ready(U)
     multiply(U, Z)
@@ -367,6 +412,7 @@
                 dma((3, 6)),
                 dma((3, 5, 2)),
                 dma((3, 5, 2)),
+                dma((3, 2)),
                 dma((3,)),
                 dma((3,)),
                 dma((2, 4, 2)),

time: 104 us -> 83.5 us (0.80)
  the two profiles are of different devices: /device:TPU:1 before, /device:TPU:103 now
where the time goes in v2:
time: 83.5 us; the launch traced here: 83.3 us
  Pallas kernels  78.6 us (94%)
  local copies, waits for them, and re-layouts  4.04 us (5%)
    pallas_call x1, Pallas kernels, body(): pl.pallas_call(functools.partial(kernel, layers, t), out_shape=[jax.Shape...  78.6 us
    unnamed x7, local copies, waits for them, and re-layouts  4.04 us

profile of v2, /device:TPU:103, one launch (start us, length us, event | category | flops | bytes accessed | tf_op | source)
XLA Modules:
  0.0 83.3 jit_solution(11434808382388636569)
XLA Ops:
  0.6 0.7 copy.5.pat_ref
  1.4 0.0 copy-start
  1.4 0.9 %copy-done = bf16[8,1,128,128]{3,2,1,0:T(8,128)(2,1)S(1)} copy-done((bf16[8,1,128,128]{3,2,1,0:T(8,128)(2,1)S(1)}, bf16[8,1,128,128]{3,2,1,0:T(8,128)(2,1)}, u32[]{:S(2)}) %copy-start) | copy-done | bytes 262168
  2.3 0.0 copy-start.1
  2.3 0.9 %copy-done.1 = bf16[8,1,128,128]{3,2,1,0:T(8,128)(2,1)S(1)} copy-done((bf16[8,1,128,128]{3,2,1,0:T(8,128)(2,1)S(1)}, bf16[8,1,128,128]{3,2,1,0:T(8,128)(2,1)}, u32[]{:S(2)}) %copy-start.1) | copy-done | bytes 262168
  3.3 78.6 %band_step.1 = (bf16[8,1,128,128]{3,2,1,0:T(8,128)(2,1)S(1)}, bf16[8,1,128,128]{3,2,1,0:T(8,128)(2,1)S(1)}) custom-call(bf16[8,1,128,128]{3,2,1,0:T(8,128)(2,1)S(1)} %copy-done, bf16[8,1,128,128]{3,2,1,0:T(8,128)(2,1)S(1)} %copy-done.1, s32[8,1]{1,0:T(8,128)S(1)} %copy.5.pat_ref), custom_call_target="tpu_custom_call" | custom-call | tf_op jit(solution)/shard_map/band_step/pallas_call | solution.py:380
  81.9 0.7 copy.8
  82.6 0.7 copy.9
Async XLA Ops:
  1.4 0.9 %copy-start = (bf16[8,1,128,128]{3,2,1,0:T(8,128)(2,1)S(1)}, bf16[8,1,128,128]{3,2,1,0:T(8,128)(2,1)}, u32[]{:S(2)}) copy-start(bf16[8,1,128,128]{3,2,1,0:T(8,128)(2,1)} %z_hbm.1) | copy-start | bytes 786436
  2.3 0.9 %copy-start.1 = (bf16[8,1,128,128]{3,2,1,0:T(8,128)(2,1)S(1)}, bf16[8,1,128,128]{3,2,1,0:T(8,128)(2,1)}, u32[]{:S(2)}) copy-start(bf16[8,1,128,128]{3,2,1,0:T(8,128)(2,1)} %y_hbm.1) | copy-start | bytes 786436

commit v3 on v2

--- a/solution.py
+++ b/solution.py
@@ -26,7 +26,7 @@
     z_hbm, y_hbm, pat_ref, w_out, x_out,
     raw, kept, marks, marks_home, left, right, lhs, rhs, prod, give, got, done, land,
     in_sem, home_send, home_recv, mark_send, mark_recv,
-    left_send, left_recv, right_send, right_recv, relay_send, pair_send, pair_recv, out_send, out_recv,
+    left_send, left_recv, right_send, right_recv, pair_send, pair_recv, out_send, out_recv,
 ):
     l = lax.axis_index("layer")
     r = lax.axis_index("rep")
@@ -165,68 +165,96 @@
     first, last = h == 0, h == 1
     edge_up, edge_down = mod(l, 4) == 3, mod(l, 4) == 0
     both = jnp.logical_and
+    either = jnp.logical_or
+    no = jnp.logical_not
+    ahead = jnp.where(first, l + 1, l - 1)
+    flat = no(either(both(first, edge_up), both(last, edge_down)))
+    flat_behind = no(either(both(first, edge_down), both(last, edge_up)))
+    cross = both(no(flat_behind), either(both(first, below), both(last, above)))
 
     def inside(n):
         row = big + n - 2
         return both(row >= 0, row < 2 * layers)
 
     def wanted(n, dl):
-        if n == 0:
-            return dl != 1
-        if n == 4:
-            return dl != 3
-        return None
-
-    def needed(n):
-        cond = inside(n)
-        want = wanted(n, delta)
-        return cond if want is None else both(cond, want)
+        return dl != (1 if n == 0 else 3)
+
+    def chunk(k, cd, kk):
+        return left.at[k, y, 2 * cd + kk]
 
     def right_start(k):
-        for d in (2, -2, 1, -1):
-            there = big + d
-            ld, hd = div(there, 2), mod(there, 2)
-            cond = both(there >= 0, there < 2 * layers)
-            want = wanted(2 - d, mod(delta + 4 - d, 4))
-            if want is not None:
-                cond = both(cond, want)
-            if d == 2:
-                cond = both(cond, jnp.logical_not(both(last, edge_up)))
-            if d == -2:
-                cond = both(cond, jnp.logical_not(both(first, edge_down)))
+        def send(at, cd, kk, n, layer, rep, cond=None):
+            remote(
+                chunk(k, cd, kk), right.at[k, n, c, kk], right_send.at[k, at + 2 * kk + cd],
+                right_recv.at[k, n, c, kk], layer, rep, cond,
+            )
+
+        for kk in (0, 1):
             for cd in range(2):
-                remote(
-                    left.at[k, y, pl.ds(2 * cd, 2)], right.at[k, 2 - d, c],
-                    right_send.at[k, 2 - d, cd], right_recv.at[k, 2 - d, c],
-                    ld, rep_of(hd, y, cd), cond,
-                )
+                send(0, cd, kk, 1 + 2 * h, l, rep_of(1 - h, y, cd))
+        for kk in (0, 1):
+            for cd in range(2):
+                send(4, cd, kk, 3 - 2 * h, jnp.where(first, l - 1, l + 1), rep_of(1 - h, y, cd), cross)
+        for kk in (1, 0):
+            for cd in range(2):
+                use = delta != 3
+                inner_up = both(last, no(edge_up))
+                cond = either(both(first, use), inner_up if kk == 1 else both(inner_up, use))
+                send(8, cd, kk, 0, l + 1, rep_of(h, y, cd), both(above, cond))
+                use = delta != 1
+                inner_down = both(first, no(edge_down))
+                cond = either(both(last, use), inner_down if kk == 1 else both(inner_down, use))
+                send(12, cd, kk, 4, l - 1, rep_of(h, y, cd), both(below, cond))
         remote(
             left.at[k, y, pl.ds(2 * other, 2)], right.at[k, 2, c],
-            right_send.at[k, 2, 0], right_recv.at[k, 2, c], l, rep_of(h, y, other),
+            right_send.at[k, 16], right_recv.at[k, 2, c, 0], l, rep_of(h, y, other),
         )
         right[k, 2, c] = left[k, y, pl.ds(2 * c, 2)]
 
     def right_relay(k):
-        for src, dst, side, step in ((1, 0, both(first, both(edge_down, below)), 3),
-                                     (3, 4, both(last, both(edge_up, above)), 1)):
+        def hand(at, n_from, n_to, cc, kk, layer, rep, cond):
+            remote(
+                right.at[k, n_from, cc, kk], right.at[k, n_to, cc, kk], right_send.at[k, at],
+                right_recv.at[k, n_to, cc, kk], layer, rep, cond,
+            )
+
+        def got_chunk(n, cc, kk, cond=None):
+            arrive(right.at[k, n, cc, kk], right_recv.at[k, n, cc, kk], cond)
+
+        def pass_on(kk):
+            step = jnp.where(first, 3, 1)
+            want = mod(delta + step, 4) != jnp.where(first, 1, 3)
             for cc in range(2):
-                arrive(right.at[k, src, cc], right_recv.at[k, src, cc], side)
-                remote(
-                    right.at[k, src, cc], right.at[k, dst, cc], relay_send.at[k, cc],
-                    right_recv.at[k, dst, cc], l, rep_of(1 - h, y, c),
-                    both(side, wanted(dst, mod(delta + step, 4))),
+                got_chunk(1 + 2 * h, cc, kk, cross)
+                hand(
+                    21 + 2 * kk + cc, 1 + 2 * h, 4 * h, cc, kk, l, rep_of(1 - h, y, c),
+                    both(cross, want),
                 )
 
+        for cc in range(2):
+            got_chunk(3 - 2 * h, cc, 0)
+            hand(17 + cc, 3 - 2 * h, 1 + 2 * h, cc, 0, ahead, rep_of(h, y, c), flat)
+        for cc in range(2):
+            got_chunk(4 - 4 * h, cc, 1, flat)
+            hand(19 + cc, 4 - 4 * h, 3 - 2 * h, cc, 1, l, rep_of(1 - h, y, c), flat)
+        pass_on(0)
+        pass_on(1)
+
     def right_ready(k):
-        arrive(right.at[k, 2, other], right_recv.at[k, 2, other])
-        for n in (1, 3, 0, 4):
-            cond = needed(n)
-            if n == 1:
-                cond = both(cond, jnp.logical_not(both(first, edge_down)))
-            if n == 3:
-                cond = both(cond, jnp.logical_not(both(last, edge_up)))
-            for cc in range(2):
-                arrive(right.at[k, n, cc], right_recv.at[k, n, cc], cond)
+        def got_chunk(n, cc, kk, cond=None):
+            arrive(right.at[k, n, cc, kk], right_recv.at[k, n, cc, kk], cond)
+
+        arrive(right.at[k, 2, other], right_recv.at[k, 2, other, 0])
+        low = both(below, delta != 1)
+        high = both(above, delta != 3)
+        for cc in range(2):
+            got_chunk(3 - 2 * h, cc, 1)
+            for kk in range(2):
+                got_chunk(1 + 2 * h, cc, kk, flat_behind)
+            got_chunk(0, cc, 0, low)
+            got_chunk(0, cc, 1, both(low, no(both(last, no(edge_down)))))
+            got_chunk(4, cc, 0, high)
+            got_chunk(4, cc, 1, both(high, no(both(first, no(edge_up)))))
 
     nothing = jnp.zeros((t, t), BF)
     apart = delta == 2
@@ -324,8 +352,8 @@
     right_start(Y)
     home_ready(Z)
     left_start(Z)
+    right_relay(Y)
     left_forward(Z)
-    right_relay(Y)
     right_start(Z)
     left_start(Y)
     for a in range(4):
@@ -410,9 +438,8 @@
                 dma((4, 2)),
                 dma((3, 6)),
                 dma((3, 6)),
-                dma((3, 5, 2)),
-                dma((3, 5, 2)),
-                dma((3, 2)),
+                dma((3, 25)),
+                dma((3, 5, 2, 2)),
                 dma((3,)),
                 dma((3,)),
                 dma((2, 4, 2)),

time: 83.5 us -> 75.9 us (0.909)
  the two profiles are of different devices: /device:TPU:103 before, /device:TPU:71 now
where the time goes in v3:
time: 75.9 us; the launch traced here: 75.7 us
  Pallas kernels  71.1 us (94%)
  local copies, waits for them, and re-layouts  4.04 us (5%)
    pallas_call x1, Pallas kernels, body(): pl.pallas_call(functools.partial(kernel, layers, t), out_shape=[jax.Shape...  71.1 us
    unnamed x7, local copies, waits for them, and re-layouts  4.04 us

profile of v3, /device:TPU:71, one launch (start us, length us, event | category | flops | bytes accessed | tf_op | source)
XLA Modules:
  0.0 75.7 jit_solution(4720412522536958448)
XLA Ops:
  0.6 0.7 copy.5.pat_ref
  1.4 0.0 copy-start
  1.4 0.9 %copy-done = bf16[8,1,128,128]{3,2,1,0:T(8,128)(2,1)S(1)} copy-done((bf16[8,1,128,128]{3,2,1,0:T(8,128)(2,1)S(1)}, bf16[8,1,128,128]{3,2,1,0:T(8,128)(2,1)}, u32[]{:S(2)}) %copy-start) | copy-done | bytes 262168
  2.3 0.0 copy-start.1
  2.3 0.9 %copy-done.1 = bf16[8,1,128,128]{3,2,1,0:T(8,128)(2,1)S(1)} copy-done((bf16[8,1,128,128]{3,2,1,0:T(8,128)(2,1)S(1)}, bf16[8,1,128,128]{3,2,1,0:T(8,128)(2,1)}, u32[]{:S(2)}) %copy-start.1) | copy-done | bytes 262168
  3.3 71.1 %band_step.1 = (bf16[8,1,128,128]{3,2,1,0:T(8,128)(2,1)S(1)}, bf16[8,1,128,128]{3,2,1,0:T(8,128)(2,1)S(1)}) custom-call(bf16[8,1,128,128]{3,2,1,0:T(8,128)(2,1)S(1)} %copy-done, bf16[8,1,128,128]{3,2,1,0:T(8,128)(2,1)S(1)} %copy-done.1, s32[8,1]{1,0:T(8,128)S(1)} %copy.5.pat_ref), custom_call_target="tpu_custom_call" | custom-call | tf_op jit(solution)/shard_map/band_step/pallas_call | solution.py:408
  74.3 0.7 copy.8
  75.0 0.7 copy.9
Async XLA Ops:
  1.4 0.9 %copy-start = (bf16[8,1,128,128]{3,2,1,0:T(8,128)(2,1)S(1)}, bf16[8,1,128,128]{3,2,1,0:T(8,128)(2,1)}, u32[]{:S(2)}) copy-start(bf16[8,1,128,128]{3,2,1,0:T(8,128)(2,1)} %z_hbm.1) | copy-start | bytes 786436
  2.3 0.9 %copy-start.1 = (bf16[8,1,128,128]{3,2,1,0:T(8,128)(2,1)S(1)}, bf16[8,1,128,128]{3,2,1,0:T(8,128)(2,1)}, u32[]{:S(2)}) copy-start(bf16[8,1,128,128]{3,2,1,0:T(8,128)(2,1)} %y_hbm.1) | copy-start | bytes 786436

commit v4 on v3

--- a/solution.py
+++ b/solution.py
@@ -24,9 +24,9 @@
 def kernel(
     layers, t,
     z_hbm, y_hbm, pat_ref, w_out, x_out,
-    raw, kept, marks, marks_home, left, right, lhs, rhs, prod, give, got, done, land,
+    raw, kept, marks, marks_home, left, right, stage, lhs, rhs, prod, give, got, done, land,
     in_sem, home_send, home_recv, mark_send, mark_recv,
-    left_send, left_recv, right_send, right_recv, pair_send, pair_recv, out_send, out_recv,
+    left_send, left_recv, right_send, right_recv, stage_recv, pair_send, pair_recv, out_send, out_recv,
 ):
     l = lax.axis_index("layer")
     r = lax.axis_index("rep")
@@ -68,12 +68,24 @@
     for load in loads:
         load.start()
 
+    above, below = l < layers - 1, l > 0
+    first, last = h == 0, h == 1
+    edge_up, edge_down = mod(l, 4) == 3, mod(l, 4) == 0
+    both = jnp.logical_and
+    either = jnp.logical_or
+    no = jnp.logical_not
+    ahead = jnp.where(first, l + 1, l - 1)
+    over = 2 * h - 1
+    flat = no(either(both(first, edge_up), both(last, edge_down)))
+    flat_behind = no(either(both(first, edge_down), both(last, edge_up)))
+    cross = both(no(flat_behind), either(both(first, below), both(last, above)))
+    carry = both(no(flat), either(both(first, l >= 4), both(last, l + 4 < layers)))
+
     barrier = pltpu.get_barrier_semaphore()
     for step in range(1, 16):
         pl.semaphore_signal(
             barrier, inc=1, device_id=(l, mod(r + step, 16)), device_id_type=MESH
         )
-    above, below = l < layers - 1, l > 0
     for near, there in ((l + 1, above), (l - 1, below)):
 
         @pl.when(there)
@@ -85,13 +97,23 @@
                     )
 
 
+    for role, hop in ((cross, -3), (carry, 3)):
+
+        @pl.when(role)
+        def _():
+            for cc in range(2):
+                for layer, hh in ((l + hop * over, h), (l + 4 * over, 1 - h)):
+                    pl.semaphore_signal(
+                        barrier, inc=1, device_id=(layer, rep_of(hh, y, cc)), device_id_type=MESH
+                    )
+
     for ap in range(8):
         marks[ap] = jnp.full((8, 128), pat_ref[ap, 0], jnp.int32)
     for k in (Z, Y):
         loads[k].wait()
         for ap in range(8):
             kept[k, ap] = jnp.where(pat_ref[ap, 0] == 1, raw[k, ap], jnp.zeros((t, t), BF))
-    peers = 15 + 4 * (above.astype(jnp.int32) + below.astype(jnp.int32))
+    peers = 15 + 4 * sum(x.astype(jnp.int32) for x in (above, below, cross, carry))
     pl.semaphore_wait(barrier, peers)
 
     def scatter(k):
@@ -162,16 +184,6 @@
         arrive(left.at[k, far, pl.ds(0, 2)], left_recv.at[k, 4])
         arrive(left.at[k, far, pl.ds(2, 2)], left_recv.at[k, 5])
 
-    first, last = h == 0, h == 1
-    edge_up, edge_down = mod(l, 4) == 3, mod(l, 4) == 0
-    both = jnp.logical_and
-    either = jnp.logical_or
-    no = jnp.logical_not
-    ahead = jnp.where(first, l + 1, l - 1)
-    flat = no(either(both(first, edge_up), both(last, edge_down)))
-    flat_behind = no(either(both(first, edge_down), both(last, edge_up)))
-    cross = both(no(flat_behind), either(both(first, below), both(last, above)))
-
     def inside(n):
         row = big + n - 2
         return both(row >= 0, row < 2 * layers)
@@ -192,19 +204,21 @@
         for kk in (0, 1):
             for cd in range(2):
                 send(0, cd, kk, 1 + 2 * h, l, rep_of(1 - h, y, cd))
-        for kk in (0, 1):
-            for cd in range(2):
-                send(4, cd, kk, 3 - 2 * h, jnp.where(first, l - 1, l + 1), rep_of(1 - h, y, cd), cross)
+        for cd in range(2):
+            send(4, cd, 0, 3 - 2 * h, l + over, rep_of(1 - h, y, cd), cross)
+            remote(
+                chunk(k, cd, 1), stage.at[k, 0, c], right_send.at[k, 6 + cd],
+                stage_recv.at[k, 0, c], l - 3 * over, rep_of(h, y, cd), cross,
+            )
+            send(25, cd, 1, 4 - 4 * h, l + over, rep_of(h, y, cd), both(cross, delta != 1 + 2 * h))
         for kk in (1, 0):
             for cd in range(2):
                 use = delta != 3
-                inner_up = both(last, no(edge_up))
-                cond = either(both(first, use), inner_up if kk == 1 else both(inner_up, use))
-                send(8, cd, kk, 0, l + 1, rep_of(h, y, cd), both(above, cond))
+                cond = either(last, use) if kk == 1 else use
+                send(8, cd, kk, 0, l + 1, rep_of(h, y, cd), both(no(edge_up), cond))
                 use = delta != 1
-                inner_down = both(first, no(edge_down))
-                cond = either(both(last, use), inner_down if kk == 1 else both(inner_down, use))
-                send(12, cd, kk, 4, l - 1, rep_of(h, y, cd), both(below, cond))
+                cond = either(first, use) if kk == 1 else use
+                send(12, cd, kk, 4, l - 1, rep_of(h, y, cd), both(no(edge_down), cond))
         remote(
             left.at[k, y, pl.ds(2 * other, 2)], right.at[k, 2, c],
             right_send.at[k, 16], right_recv.at[k, 2, c, 0], l, rep_of(h, y, other),
@@ -220,6 +234,15 @@
 
         def got_chunk(n, cc, kk, cond=None):
             arrive(right.at[k, n, cc, kk], right_recv.at[k, n, cc, kk], cond)
+
+        def carried(which, kk, n, cond):
+            for cc in range(2):
+                arrive(stage.at[k, which, cc], stage_recv.at[k, which, cc], cond)
+                remote(
+                    stage.at[k, which, cc], right.at[k, n, cc, kk],
+                    right_send.at[k, 33 + 2 * which + cc], right_recv.at[k, n, cc, kk],
+                    l + 4 * over, rep_of(1 - h, y, c), cond,
+                )
 
         def pass_on(kk):
             step = jnp.where(first, 3, 1)
@@ -231,14 +254,23 @@
                     both(cross, want),
                 )
 
+        near = both(cross, delta != 2)
         for cc in range(2):
             got_chunk(3 - 2 * h, cc, 0)
             hand(17 + cc, 3 - 2 * h, 1 + 2 * h, cc, 0, ahead, rep_of(h, y, c), flat)
+            remote(
+                right.at[k, 3 - 2 * h, cc, 0], stage.at[k, 1, cc], right_send.at[k, 29 + cc],
+                stage_recv.at[k, 1, cc], l - 3 * over, rep_of(h, y, c), near,
+            )
+        pass_on(0)
+        carried(0, 1, 3 - 2 * h, carry)
         for cc in range(2):
             got_chunk(4 - 4 * h, cc, 1, flat)
             hand(19 + cc, 4 - 4 * h, 3 - 2 * h, cc, 1, l, rep_of(1 - h, y, c), flat)
-        pass_on(0)
-        pass_on(1)
+        for cc in range(2):
+            got_chunk(3 - 2 * h, cc, 1, cross)
+            hand(31 + cc, 3 - 2 * h, 4 - 4 * h, cc, 1, l + over, rep_of(1 - h, y, c), near)
+        carried(1, 0, 4 - 4 * h, both(carry, delta != 0))
 
     def right_ready(k):
         def got_chunk(n, cc, kk, cond=None):
@@ -248,9 +280,9 @@
         low = both(below, delta != 1)
         high = both(above, delta != 3)
         for cc in range(2):
-            got_chunk(3 - 2 * h, cc, 1)
-            for kk in range(2):
-                got_chunk(1 + 2 * h, cc, kk, flat_behind)
+            got_chunk(3 - 2 * h, cc, 1, no(cross))
+            got_chunk(1 + 2 * h, cc, 0, flat_behind)
+            got_chunk(1 + 2 * h, cc, 1, either(flat_behind, cross))
             got_chunk(0, cc, 0, low)
             got_chunk(0, cc, 1, both(low, no(both(last, no(edge_down)))))
             got_chunk(4, cc, 0, high)
@@ -424,6 +456,7 @@
                 pltpu.VMEM((4, 2, 8, 128), jnp.int32),
                 pltpu.VMEM((3, 4, 4, 2, t, t), BF),
                 pltpu.VMEM((3, 5, 2, 2, 2, t, t), BF),
+                pltpu.VMEM((3, 2, 2, 2, t, t), BF),
                 pltpu.VMEM((2, 4 * t, 6 * t), BF),
                 pltpu.VMEM((2, 6 * t, 4 * t), BF),
                 pltpu.VMEM((2, 4, 4, t, t), F32),
@@ -438,8 +471,9 @@
                 dma((4, 2)),
                 dma((3, 6)),
                 dma((3, 6)),
-                dma((3, 25)),
+                dma((3, 37)),
                 dma((3, 5, 2, 2)),
+                dma((3, 2, 2)),
                 dma((3,)),
                 dma((3,)),
                 dma((2, 4, 2)),

time: 75.9 us -> 72.9 us (0.960)
  the two profiles are of different devices: /device:TPU:71 before, /device:TPU:72 now
where the time goes in v4:
time: 72.9 us; the launch traced here: 72.8 us
  Pallas kernels  68.1 us (93%)
  local copies, waits for them, and re-layouts  4.04 us (6%)
    pallas_call x1, Pallas kernels, body(): pl.pallas_call(functools.partial(kernel, layers, t), out_shape=[jax.Shape...  68.1 us
    unnamed x7, local copies, waits for them, and re-layouts  4.04 us

profile of v4, /device:TPU:72, one launch (start us, length us, event | category | flops | bytes accessed | tf_op | source)
XLA Modules:
  0.0 72.8 jit_solution(11914865095479799285)
XLA Ops:
  0.6 0.7 %copy.5.pat_ref = s32[8,1]{1,0:T(8,128)S(1)} copy(s32[8,1]{0,1:T(1,128)} %param.5) | data formatting | bytes 64 | tf_op args[2]
  1.4 0.0 copy-start
  1.4 0.9 %copy-done = bf16[8,1,128,128]{3,2,1,0:T(8,128)(2,1)S(1)} copy-done((bf16[8,1,128,128]{3,2,1,0:T(8,128)(2,1)S(1)}, bf16[8,1,128,128]{3,2,1,0:T(8,128)(2,1)}, u32[]{:S(2)}) %copy-start) | copy-done | bytes 262168
  2.3 0.0 copy-start.1
  2.3 0.9 %copy-done.1 = bf16[8,1,128,128]{3,2,1,0:T(8,128)(2,1)S(1)} copy-done((bf16[8,1,128,128]{3,2,1,0:T(8,128)(2,1)S(1)}, bf16[8,1,128,128]{3,2,1,0:T(8,128)(2,1)}, u32[]{:S(2)}) %copy-start.1) | copy-done | bytes 262168
  3.3 68.1 %band_step.1 = (bf16[8,1,128,128]{3,2,1,0:T(8,128)(2,1)S(1)}, bf16[8,1,128,128]{3,2,1,0:T(8,128)(2,1)S(1)}) custom-call(bf16[8,1,128,128]{3,2,1,0:T(8,128)(2,1)S(1)} %copy-done, bf16[8,1,128,128]{3,2,1,0:T(8,128)(2,1)S(1)} %copy-done.1, s32[8,1]{1,0:T(8,128)S(1)} %copy.5.pat_ref), custom_call_target="tpu_custom_call" | custom-call | tf_op jit(solution)/shard_map/band_step/pallas_call | solution.py:440
  71.3 0.7 copy.8
  72.1 0.7 copy.9
Async XLA Ops:
  1.4 0.9 %copy-start = (bf16[8,1,128,128]{3,2,1,0:T(8,128)(2,1)S(1)}, bf16[8,1,128,128]{3,2,1,0:T(8,128)(2,1)}, u32[]{:S(2)}) copy-start(bf16[8,1,128,128]{3,2,1,0:T(8,128)(2,1)} %z_hbm.1) | copy-start | bytes 786436
  2.3 0.9 %copy-start.1 = (bf16[8,1,128,128]{3,2,1,0:T(8,128)(2,1)S(1)}, bf16[8,1,128,128]{3,2,1,0:T(8,128)(2,1)}, u32[]{:S(2)}) copy-start(bf16[8,1,128,128]{3,2,1,0:T(8,128)(2,1)} %y_hbm.1) | copy-start | bytes 786436

commit v5 on v4

--- a/solution.py
+++ b/solution.py
@@ -24,9 +24,9 @@
 def kernel(
     layers, t,
     z_hbm, y_hbm, pat_ref, w_out, x_out,
-    raw, kept, marks, marks_home, left, right, stage, lhs, rhs, prod, give, got, done, land,
+    raw, kept, marks, marks_home, left, right, stage, lhs, rhs, prod, give, got, done,
     in_sem, home_send, home_recv, mark_send, mark_recv,
-    left_send, left_recv, right_send, right_recv, stage_recv, pair_send, pair_recv, out_send, out_recv,
+    left_send, left_recv, right_send, right_recv, stage_recv, pair_send, pair_recv, out_send, out_recv, self_sem,
 ):
     l = lax.axis_index("layer")
     r = lax.axis_index("rep")
@@ -36,6 +36,7 @@
     delta = mod(y + 4 * layers * 2 - big, 4)
     other = 1 - c
     pending = []
+    kept_here = []
 
     def rep_of(hh, yy, cc):
         return hh * 8 + yy * 2 + cc
@@ -108,16 +109,16 @@
                     )
 
     for ap in range(8):
-        marks[ap] = jnp.full((8, 128), pat_ref[ap, 0], jnp.int32)
+        marks[ap] = jnp.full((8, 128), pat_ref[ap], jnp.int32)
     for k in (Z, Y):
         loads[k].wait()
         for ap in range(8):
-            kept[k, ap] = jnp.where(pat_ref[ap, 0] == 1, raw[k, ap], jnp.zeros((t, t), BF))
+            kept[k, ap] = jnp.where(pat_ref[ap] == 1, raw[k, ap], jnp.zeros((t, t), BF))
     peers = 15 + 4 * sum(x.astype(jnp.int32) for x in (above, below, cross, carry))
     pl.semaphore_wait(barrier, peers)
 
     def scatter(k):
-        for ap in range(8):
+        for ap in (0, 4, 2, 6, 1, 5, 3, 7):
             jm = mod(shift + ap + r, 16)
             yd, cd, b2 = div(jm, 4), div(mod(jm, 4), 2), mod(jm, 2)
             dest = rep_of(ap // 4, yd, cd)
@@ -144,8 +145,8 @@
         source = mod(4 * y + 2 * c + b2 - shift - (4 * h + a) + 32, 16)
         return source != r
 
-    def home_ready(k):
-        for a in range(4):
+    def home_ready(k, rows=(0, 1, 2, 3)):
+        for a in rows:
             for b2 in range(2):
                 arrive(left.at[k, y, a, b2], home_recv.at[k, a, b2], from_other(a, b2))
 
@@ -194,16 +195,23 @@
     def chunk(k, cd, kk):
         return left.at[k, y, 2 * cd + kk]
 
-    def right_start(k):
+    def right_start(k, rows_of=None):
+        def home(*rows):
+            if rows_of is not None:
+                rows_of(k, rows)
+
         def send(at, cd, kk, n, layer, rep, cond=None):
             remote(
                 chunk(k, cd, kk), right.at[k, n, c, kk], right_send.at[k, at + 2 * kk + cd],
                 right_recv.at[k, n, c, kk], layer, rep, cond,
             )
 
-        for kk in (0, 1):
-            for cd in range(2):
-                send(0, cd, kk, 1 + 2 * h, l, rep_of(1 - h, y, cd))
+        for cd in range(2):
+            home(2 * cd)
+            send(0, cd, 0, 1 + 2 * h, l, rep_of(1 - h, y, cd))
+        home(1, 3)
+        for cd in range(2):
+            send(0, cd, 1, 1 + 2 * h, l, rep_of(1 - h, y, cd))
         for cd in range(2):
             send(4, cd, 0, 3 - 2 * h, l + over, rep_of(1 - h, y, cd), cross)
             remote(
@@ -225,7 +233,7 @@
         )
         right[k, 2, c] = left[k, y, pl.ds(2 * c, 2)]
 
-    def right_relay(k):
+    def right_relay(k, parts=(0, 1, 2)):
         def hand(at, n_from, n_to, cc, kk, layer, rep, cond):
             remote(
                 right.at[k, n_from, cc, kk], right.at[k, n_to, cc, kk], right_send.at[k, at],
@@ -255,22 +263,21 @@
                 )
 
         near = both(cross, delta != 2)
-        for cc in range(2):
-            got_chunk(3 - 2 * h, cc, 0)
-            hand(17 + cc, 3 - 2 * h, 1 + 2 * h, cc, 0, ahead, rep_of(h, y, c), flat)
-            remote(
-                right.at[k, 3 - 2 * h, cc, 0], stage.at[k, 1, cc], right_send.at[k, 29 + cc],
-                stage_recv.at[k, 1, cc], l - 3 * over, rep_of(h, y, c), near,
-            )
-        pass_on(0)
-        carried(0, 1, 3 - 2 * h, carry)
-        for cc in range(2):
-            got_chunk(4 - 4 * h, cc, 1, flat)
-            hand(19 + cc, 4 - 4 * h, 3 - 2 * h, cc, 1, l, rep_of(1 - h, y, c), flat)
-        for cc in range(2):
-            got_chunk(3 - 2 * h, cc, 1, cross)
-            hand(31 + cc, 3 - 2 * h, 4 - 4 * h, cc, 1, l + over, rep_of(1 - h, y, c), near)
-        carried(1, 0, 4 - 4 * h, both(carry, delta != 0))
+        if 0 in parts:
+            for cc in range(2):
+                got_chunk(3 - 2 * h, cc, 0)
+                hand(17 + cc, 3 - 2 * h, 1 + 2 * h, cc, 0, ahead, rep_of(h, y, c), flat)
+                hand(29 + cc, 3 - 2 * h, 4 - 4 * h, cc, 0, l + over, rep_of(1 - h, y, c), near)
+            pass_on(0)
+        if 1 in parts:
+            carried(0, 1, 3 - 2 * h, carry)
+            for cc in range(2):
+                got_chunk(4 - 4 * h, cc, 1, flat)
+                hand(19 + cc, 4 - 4 * h, 3 - 2 * h, cc, 1, l, rep_of(1 - h, y, c), flat)
+        if 2 in parts:
+            for cc in range(2):
+                got_chunk(3 - 2 * h, cc, 1, cross)
+                hand(31 + cc, 3 - 2 * h, 4 - 4 * h, cc, 1, l + over, rep_of(1 - h, y, c), near)
 
     def right_ready(k):
         def got_chunk(n, cc, kk, cond=None):
@@ -293,11 +300,10 @@
     toward = jnp.where(delta == 3, -1, delta)
     middle = (jnp.where(apart, -2, toward), jnp.where(apart, 2, toward))
 
-    def multiply(kl, kr):
+    def build_left(kl):
         for s in range(2):
             for at, n in enumerate((0, 1, 2) if s == 0 else (2, 3, 4)):
                 cls = mod(big + n + 2, 4)
-                gap = middle[s] - (n - 2)
                 for kk in range(2):
                     inner = 2 * c + kk
                     for a in range(4):
@@ -307,6 +313,15 @@
                         if n == 4:
                             tile = jnp.where(inner < a, tile, nothing)
                         lhs[s, a * t:(a + 1) * t, (2 * at + kk) * t:(2 * at + kk + 1) * t] = tile
+
+    def build_right(kr, rows):
+        for s in range(2):
+            for at, n in enumerate((0, 1, 2) if s == 0 else (2, 3, 4)):
+                if n not in rows:
+                    continue
+                gap = middle[s] - (n - 2)
+                for kk in range(2):
+                    inner = 2 * c + kk
                     for b in range(4):
                         whole = jnp.logical_and(gap >= -1, gap <= 1)
                         low = jnp.logical_and(gap == 2, b < inner)
@@ -317,113 +332,126 @@
                         if s == 1 and n == 2:
                             good = jnp.logical_and(good, apart)
                         tile = jnp.where(good, right[kr, n, b // 2, kk, b % 2], nothing)
-                        rhs[s, (2 * at + kk) * t:(2 * at + kk + 1) * t, b * t:(b + 1) * t] = tile
-        for s in range(2):
-            for half in range(2):
-                out = jnp.dot(
-                    lhs[s], rhs[s, :, half * 2 * t:(half + 1) * 2 * t], preferred_element_type=F32
-                )
-                for a in range(4):
-                    for b2 in range(2):
-                        prod[s, a, 2 * half + b2] = out[a * t:(a + 1) * t, b2 * t:(b2 + 1) * t]
-
-    def total(a, b):
-        first = jnp.logical_or(jnp.logical_not(apart), b >= a)
-        second = jnp.logical_or(jnp.logical_not(apart), b < a)
-        empty = jnp.zeros((t, t), F32)
-        return jnp.where(first, prod[0, a, b], empty) + jnp.where(second, prod[1, a, b], empty)
-
-    def share(k):
+                        rhs[s, b // 2, (2 * at + kk) * t:(2 * at + kk + 1) * t, (b % 2) * t:(b % 2 + 1) * t] = tile
+
+    def columns(half):
+        first_out = jnp.dot(lhs[0], rhs[0, half], preferred_element_type=F32)
+        second_out = jnp.dot(lhs[1], rhs[1, half], preferred_element_type=F32)
+
+        def value(a, b2):
+            b = 2 * half + b2
+            use_first = either(no(apart), b >= a)
+            use_second = either(no(apart), b < a)
+            empty = jnp.zeros((t, t), F32)
+            x = first_out[a * t:(a + 1) * t, b2 * t:(b2 + 1) * t]
+            z = second_out[a * t:(a + 1) * t, b2 * t:(b2 + 1) * t]
+            return jnp.where(use_first, x, empty) + jnp.where(use_second, z, empty)
+
+        return value
+
+    def multiply(k):
+        part = columns(other)
         for a in range(4):
             for b2 in range(2):
-                give[k, a, b2] = total(a, 2 * other + b2).astype(BF)
-                prod[0, a, 2 * c + b2] = total(a, 2 * c + b2)
+                give[k, a, b2] = part(a, b2).astype(BF)
         remote(
             give.at[k], got.at[k], pair_send.at[k], pair_recv.at[k], l, rep_of(h, y, other)
         )
+        part = columns(c)
+        for a in range(4):
+            for b2 in range(2):
+                prod[a, b2] = part(a, b2)
 
     def summed(k, a, b2):
-        value = prod[0, a, 2 * c + b2] + got[k, a, b2].astype(F32)
+        value = prod[a, b2] + got[k, a, b2].astype(F32)
         return value
 
     def marked(a, b2):
         return marks_home[a, b2][0:1, :] == 1
 
-    def owner_send(k):
+    def owner_send(k, out_ref):
         for a in range(4):
             for b2 in range(2):
-                slot = mod(4 * y + 2 * c + b2 + shift - (4 * h + a) + 32, 16)
                 done[k, a, b2] = jnp.where(
                     marked(a, b2), summed(k, a, b2), jnp.zeros((t, t), F32)
                 ).astype(BF)
         for a in range(4):
             for b2 in range(2):
                 slot = mod(4 * y + 2 * c + b2 + shift - (4 * h + a) + 32, 16)
-                here, away = slot == r, slot != r
-
-                @pl.when(here)
-                def _():
-                    land[k, 4 * h + a] = done[k, a, b2]
-
+                here = slot == r
+                mine = pltpu.make_async_copy(
+                    done.at[k, a, b2], out_ref.at[4 * h + a, 0], self_sem.at[k, a, b2]
+                )
+                pl.when(here)(mine.start)
+                kept_here.append((here, mine))
                 remote(
-                    done.at[k, a, b2], land.at[k, 4 * h + a], out_send.at[k, a, b2],
-                    out_recv.at[k, 4 * h + a], l, slot, away,
+                    done.at[k, a, b2], out_ref.at[4 * h + a, 0], out_send.at[k, a, b2],
+                    out_recv.at[k, 4 * h + a], l, slot, slot != r,
                 )
 
     def owner_ready(k, out_ref):
         for ap in range(8):
             jm = mod(shift + ap + r, 16)
             source = rep_of(ap // 4, div(jm, 4), div(mod(jm, 4), 2))
-            arrive(land.at[k, ap], out_recv.at[k, ap], source != r)
-        for ap in range(8):
-            out_ref[ap, 0] = land[k, ap]
+            arrive(out_ref.at[ap, 0], out_recv.at[k, ap], source != r)
+
+    def marks_ready():
+        for a in range(4):
+            for b2 in range(2):
+                arrive(marks_home.at[a, b2], mark_recv.at[a, b2], from_other(a, b2))
+
+    def finish_u():
+        arrive(got.at[U], pair_recv.at[U])
+        rows = lax.broadcasted_iota(jnp.int32, (t, t), 0)
+        cols = lax.broadcasted_iota(jnp.int32, (t, t), 1)
+        for a in range(4):
+            for b2 in range(2):
+                on = jnp.logical_and(mod(big, 4) == y, 2 * c + b2 == a)
+                eye = jnp.where(rows == cols, jnp.where(on, F32(1.5), F32(0.0)), F32(0.0))
+                value = eye - 0.5 * summed(U, a, b2)
+                left[U, y, a, b2] = jnp.where(marked(a, b2), value, jnp.zeros((t, t), F32)).astype(BF)
 
     scatter(Y)
     scatter(Z)
-    home_ready(Y)
-    right_start(Y)
+    right_start(Y, home_ready)
     home_ready(Z)
     left_start(Z)
-    right_relay(Y)
+    right_relay(Y, (0,))
     left_forward(Z)
+    right_relay(Y, (1, 2))
     right_start(Z)
     left_start(Y)
-    for a in range(4):
-        for b2 in range(2):
-            arrive(marks_home.at[a, b2], mark_recv.at[a, b2], from_other(a, b2))
+    marks_ready()
     left_ready(Z)
+    build_left(Z)
     right_ready(Y)
-    multiply(Z, Y)
-    share(U)
+    build_right(Y, (0, 1, 2, 3, 4))
+    multiply(U)
     left_forward(Y)
     right_relay(Z)
-    arrive(got.at[U], pair_recv.at[U])
-    rows = lax.broadcasted_iota(jnp.int32, (t, t), 0)
-    cols = lax.broadcasted_iota(jnp.int32, (t, t), 1)
-    for a in range(4):
-        for b2 in range(2):
-            on = jnp.logical_and(mod(big, 4) == y, 2 * c + b2 == a)
-            eye = jnp.where(rows == cols, jnp.where(on, F32(1.5), F32(0.0)), F32(0.0))
-            value = eye - 0.5 * summed(U, a, b2)
-            left[U, y, a, b2] = jnp.where(marked(a, b2), value, jnp.zeros((t, t), F32)).astype(BF)
+    finish_u()
     left_start(U)
     right_start(U)
     left_forward(U)
     right_relay(U)
     right_ready(Z)
+    build_right(Z, (0, 1, 2, 3, 4))
     left_ready(U)
-    multiply(U, Z)
-    share(Z)
+    build_left(U)
+    multiply(Z)
     arrive(got.at[Z], pair_recv.at[Z])
-    owner_send(Z)
+    owner_send(Z, w_out)
     left_ready(Y)
+    build_left(Y)
     right_ready(U)
-    multiply(Y, U)
-    share(Y)
+    build_right(U, (0, 1, 2, 3, 4))
+    multiply(Y)
     arrive(got.at[Y], pair_recv.at[Y])
-    owner_send(Y)
+    owner_send(Y, x_out)
     owner_ready(Z, w_out)
     owner_ready(Y, x_out)
+    for cond, copy in kept_here:
+        pl.when(cond)(copy.wait)
     for cond, copy in pending:
         if cond is None:
             copy.wait_send()
@@ -448,7 +476,7 @@
                 pl.BlockSpec(memory_space=pl.ANY),
                 pl.BlockSpec(memory_space=pltpu.SMEM),
             ],
-            out_specs=[pl.BlockSpec(memory_space=pltpu.VMEM)] * 2,
+            out_specs=[pl.BlockSpec(memory_space=pl.ANY)] * 2,
             scratch_shapes=[
                 pltpu.VMEM((2, 8, t, t), BF),
                 pltpu.VMEM((2, 8, t, t), BF),
@@ -458,12 +486,11 @@
                 pltpu.VMEM((3, 5, 2, 2, 2, t, t), BF),
                 pltpu.VMEM((3, 2, 2, 2, t, t), BF),
                 pltpu.VMEM((2, 4 * t, 6 * t), BF),
-                pltpu.VMEM((2, 6 * t, 4 * t), BF),
-                pltpu.VMEM((2, 4, 4, t, t), F32),
+                pltpu.VMEM((2, 2, 6 * t, 2 * t), BF),
+                pltpu.VMEM((4, 2, t, t), F32),
                 pltpu.VMEM((3, 4, 2, t, t), BF),
                 pltpu.VMEM((3, 4, 2, t, t), BF),
                 pltpu.VMEM((2, 4, 2, t, t), BF),
-                pltpu.VMEM((2, 8, t, t), BF),
                 dma((2,)),
                 dma((2, 8)),
                 dma((2, 4, 2)),
@@ -478,12 +505,13 @@
                 dma((3,)),
                 dma((2, 4, 2)),
                 dma((2, 8)),
+                dma((2, 4, 2)),
             ],
             compiler_params=pltpu.CompilerParams(
-                collective_id=0, has_side_effects=True, vmem_limit_bytes=40 * 1024 * 1024
+                collective_id=0, has_side_effects=True, vmem_limit_bytes=67043328
             ),
             name="band_step",
-        )(inverse_root, square_root, pattern)
+        )(inverse_root, square_root, pattern.reshape(-1))
 
     return jax.shard_map(
         body,

time: 72.9 us -> 68.1 us (0.934)
  the two profiles are of different devices: /device:TPU:72 before, /device:TPU:71 now
where the time goes in v5:
time: 68.1 us; the launch traced here: 68 us
  Pallas kernels  64.9 us (95%)
  local copies, waits for them, and re-layouts  2.42 us (4%)
    pallas_call x1, Pallas kernels, body(): pl.pallas_call(functools.partial(kernel, layers, t), out_shape=[jax.Shape...  64.9 us
    unnamed x4, local copies, waits for them, and re-layouts  2.42 us

profile of v5, /device:TPU:71, one launch (start us, length us, event | category | flops | bytes accessed | tf_op | source)
XLA Modules:
  0.0 68.0 jit_solution(13601606750045329656)
XLA Ops:
  0.6 64.9 %band_step.1 = (bf16[8,1,128,128]{3,2,1,0:T(8,128)(2,1)}, bf16[8,1,128,128]{3,2,1,0:T(8,128)(2,1)}) custom-call(bf16[8,1,128,128]{3,2,1,0:T(8,128)(2,1)} %z_hbm.1, bf16[8,1,128,128]{3,2,1,0:T(8,128)(2,1)} %y_hbm.1, s32[8]{0:T(128)} %bitcast.1), custom_call_target="tpu_custom_call" | custom-call | tf_op jit(solution)/shard_map/band_step/pallas_call | solution.py:468
  65.6 0.0 copy-start
  65.6 1.7 %copy.7 = bf16[8,1,128,128]{3,2,1,0:T(8,128)(2,1)} copy(bf16[8,1,128,128]{3,2,1,0:T(8,128)(2,1)} %get-tuple-element.4) | data formatting | bytes 524288
  67.3 0.0 copy-done
  67.3 0.7 %copy.8 = bf16[8,1,128,128]{3,2,1,0:T(8,128)(2,1)} copy(bf16[8,1,128,128]{3,2,1,0:T(8,128)(2,1)S(1)} %copy-done) | data formatting | bytes 524288
Async XLA Ops:
  65.6 1.7 %copy-start = (bf16[8,1,128,128]{3,2,1,0:T(8,128)(2,1)S(1)}, bf16[8,1,128,128]{3,2,1,0:T(8,128)(2,1)}, u32[]{:S(2)}) copy-start(bf16[8,1,128,128]{3,2,1,0:T(8,128)(2,1)} %get-tuple-element.5) | copy-start | bytes 786436

commit v6 on v5

--- a/solution.py
+++ b/solution.py
@@ -23,8 +23,8 @@
 
 def kernel(
     layers, t,
-    z_hbm, y_hbm, pat_ref, w_out, x_out,
-    raw, kept, marks, marks_home, left, right, stage, lhs, rhs, prod, give, got, done,
+    z_hbm, y_hbm, pat_hbm, w_out, x_out,
+    pat_ref, raw, kept, marks, marks_home, left, right, stage, lhs, rhs, prod, give, got, done,
     in_sem, home_send, home_recv, mark_send, mark_recv,
     left_send, left_recv, right_send, right_recv, stage_recv, pair_send, pair_recv, out_send, out_recv, self_sem,
 ):
@@ -50,6 +50,12 @@
             copy.start()
         else:
             pl.when(cond)(copy.start)
+
+    def settle(size, send_sem, cond=None):
+        copy = pltpu.make_async_remote_copy(
+            src_ref=size, dst_ref=size, send_sem=send_sem, recv_sem=send_sem,
+            device_id=(l, r), device_id_type=MESH,
+        )
         pending.append((cond, copy))
 
     def arrive(dst, recv_sem, cond=None):
@@ -66,6 +72,8 @@
         pltpu.make_async_copy(ref.at[:, 0], raw.at[k], in_sem.at[k])
         for k, ref in ((Z, z_hbm), (Y, y_hbm))
     ]
+    pat_load = pltpu.make_async_copy(pat_hbm, pat_ref, in_sem.at[2])
+    pat_load.start()
     for load in loads:
         load.start()
 
@@ -108,6 +116,7 @@
                         barrier, inc=1, device_id=(layer, rep_of(hh, y, cc)), device_id_type=MESH
                     )
 
+    pat_load.wait()
     for ap in range(8):
         marks[ap] = jnp.full((8, 128), pat_ref[ap], jnp.int32)
     for k in (Z, Y):
@@ -117,10 +126,27 @@
     peers = 15 + 4 * sum(x.astype(jnp.int32) for x in (above, below, cross, carry))
     pl.semaphore_wait(barrier, peers)
 
+    def home_of(ap):
+        jm = mod(shift + ap + r, 16)
+        return div(jm, 4), div(mod(jm, 4), 2), mod(jm, 2)
+
+    def to_rep(ap):
+        yd, cd, _ = home_of(ap)
+        return rep_of(ap // 4, yd, cd)
+
+    staying = sum((to_rep(ap) == r).astype(jnp.int32) for ap in range(8))
+
+    def moved(ref, sem):
+        for n in (6, 7, 8):
+            settle(ref.at[pl.ds(0, n)], sem, 8 - staying == n)
+
+    def arrived(ref, sem):
+        for n in (6, 7, 8):
+            arrive(ref.at[pl.ds(0, n)], sem, 8 - staying == n)
+
     def scatter(k):
         for ap in (0, 4, 2, 6, 1, 5, 3, 7):
-            jm = mod(shift + ap + r, 16)
-            yd, cd, b2 = div(jm, 4), div(mod(jm, 4), 2), mod(jm, 2)
+            yd, cd, b2 = home_of(ap)
             dest = rep_of(ap // 4, yd, cd)
             here, away = dest == r, dest != r
             a = ap % 4
@@ -132,58 +158,45 @@
                     marks_home[a, b2] = marks[ap]
 
             remote(
-                kept.at[k, ap], left.at[k, yd, a, b2], home_send.at[k, ap],
-                home_recv.at[k, a, b2], l, dest, away,
+                kept.at[k, ap], left.at[k, yd, a, b2], home_send.at[k], home_recv.at[k],
+                l, dest, away,
             )
             if k == Y:
                 remote(
-                    marks.at[ap], marks_home.at[a, b2], mark_send.at[ap],
-                    mark_recv.at[a, b2], l, dest, away,
+                    marks.at[ap], marks_home.at[a, b2], mark_send, mark_recv, l, dest, away
                 )
-
-    def from_other(a, b2):
-        source = mod(4 * y + 2 * c + b2 - shift - (4 * h + a) + 32, 16)
-        return source != r
-
-    def home_ready(k, rows=(0, 1, 2, 3)):
-        for a in rows:
-            for b2 in range(2):
-                arrive(left.at[k, y, a, b2], home_recv.at[k, a, b2], from_other(a, b2))
+        moved(kept.at[k], home_send.at[k])
+        if k == Y:
+            moved(marks, mark_send)
+
+    def home_ready(k):
+        arrived(kept.at[k], home_recv.at[k])
 
     up, down = mod(y + 1, 4), mod(y + 3, 4)
     far = mod(y + 2, 4)
 
+    def half_of(k, whose, half):
+        return left.at[k, whose, pl.ds(2 * half, 2)]
+
+    def left_send_half(k, whose, half, at, to):
+        part = half_of(k, whose, half)
+        remote(part, part, left_send.at[k], left_recv.at[k, at], l, rep_of(h, to, c))
+
     def left_start(k):
-        for step, half in ((0, 0), (1, 1)):
-            part = pl.ds(2 * half, 2)
-            remote(
-                left.at[k, y, part], left.at[k, y, part], left_send.at[k, half],
-                left_recv.at[k, half], l, rep_of(h, up, c),
-            )
-            back = 1 - half
-            part = pl.ds(2 * back, 2)
-            remote(
-                left.at[k, y, part], left.at[k, y, part], left_send.at[k, 2 + back],
-                left_recv.at[k, 2 + back], l, rep_of(h, down, c),
-            )
+        left_send_half(k, y, 0, 0, up)
+        left_send_half(k, y, 1, 1, down)
+        left_send_half(k, y, 1, 2, up)
+        left_send_half(k, y, 0, 2, down)
+        settle(left.at[k, pl.ds(0, 3)], left_send.at[k])
 
     def left_forward(k):
-        arrive(left.at[k, down, pl.ds(0, 2)], left_recv.at[k, 0])
-        remote(
-            left.at[k, down, pl.ds(0, 2)], left.at[k, down, pl.ds(0, 2)], left_send.at[k, 4],
-            left_recv.at[k, 4], l, rep_of(h, up, c),
-        )
-        arrive(left.at[k, up, pl.ds(2, 2)], left_recv.at[k, 3])
-        remote(
-            left.at[k, up, pl.ds(2, 2)], left.at[k, up, pl.ds(2, 2)], left_send.at[k, 5],
-            left_recv.at[k, 5], l, rep_of(h, down, c),
-        )
+        arrive(half_of(k, down, 0), left_recv.at[k, 0])
+        left_send_half(k, down, 0, 2, up)
+        arrive(half_of(k, up, 1), left_recv.at[k, 1])
+        left_send_half(k, up, 1, 2, down)
 
     def left_ready(k):
-        arrive(left.at[k, down, pl.ds(2, 2)], left_recv.at[k, 1])
-        arrive(left.at[k, up, pl.ds(0, 2)], left_recv.at[k, 2])
-        arrive(left.at[k, far, pl.ds(0, 2)], left_recv.at[k, 4])
-        arrive(left.at[k, far, pl.ds(2, 2)], left_recv.at[k, 5])
+        arrive(left.at[k, pl.ds(0, 2)], left_recv.at[k, 2])
 
     def inside(n):
         row = big + n - 2
@@ -195,105 +208,97 @@
     def chunk(k, cd, kk):
         return left.at[k, y, 2 * cd + kk]
 
-    def right_start(k, rows_of=None):
-        def home(*rows):
-            if rows_of is not None:
-                rows_of(k, rows)
+    def right_start(k):
+        four, eight = left.at[k, y, pl.ds(0, 2)], left.at[k, y]
 
         def send(at, cd, kk, n, layer, rep, cond=None):
             remote(
-                chunk(k, cd, kk), right.at[k, n, c, kk], right_send.at[k, at + 2 * kk + cd],
-                right_recv.at[k, n, c, kk], layer, rep, cond,
+                chunk(k, cd, kk), right.at[k, n, c, kk], right_send.at[k, at],
+                right_recv.at[k, n, kk], layer, rep, cond,
             )
 
+        for kk in (0, 1):
+            for cd in range(2):
+                send(0, cd, kk, 1 + 2 * h, l, rep_of(1 - h, y, cd))
+        settle(eight, right_send.at[k, 0])
+        direct = both(cross, delta != 1 + 2 * h)
         for cd in range(2):
-            home(2 * cd)
-            send(0, cd, 0, 1 + 2 * h, l, rep_of(1 - h, y, cd))
-        home(1, 3)
-        for cd in range(2):
-            send(0, cd, 1, 1 + 2 * h, l, rep_of(1 - h, y, cd))
-        for cd in range(2):
-            send(4, cd, 0, 3 - 2 * h, l + over, rep_of(1 - h, y, cd), cross)
+            send(1, cd, 0, 3 - 2 * h, l + over, rep_of(1 - h, y, cd), cross)
             remote(
-                chunk(k, cd, 1), stage.at[k, 0, c], right_send.at[k, 6 + cd],
-                stage_recv.at[k, 0, c], l - 3 * over, rep_of(h, y, cd), cross,
+                chunk(k, cd, 1), stage.at[k, c], right_send.at[k, 1],
+                stage_recv.at[k], l - 3 * over, rep_of(h, y, cd), cross,
             )
-            send(25, cd, 1, 4 - 4 * h, l + over, rep_of(h, y, cd), both(cross, delta != 1 + 2 * h))
+            send(2, cd, 1, 4 - 4 * h, l + over, rep_of(h, y, cd), direct)
+        settle(eight, right_send.at[k, 1], cross)
+        settle(four, right_send.at[k, 2], direct)
         for kk in (1, 0):
+            use = delta != 3
+            up_cond = both(no(edge_up), either(last, use) if kk == 1 else use)
+            use = delta != 1
+            down_cond = both(no(edge_down), either(first, use) if kk == 1 else use)
             for cd in range(2):
-                use = delta != 3
-                cond = either(last, use) if kk == 1 else use
-                send(8, cd, kk, 0, l + 1, rep_of(h, y, cd), both(no(edge_up), cond))
-                use = delta != 1
-                cond = either(first, use) if kk == 1 else use
-                send(12, cd, kk, 4, l - 1, rep_of(h, y, cd), both(no(edge_down), cond))
+                send(3 + kk, cd, kk, 0, l + 1, rep_of(h, y, cd), up_cond)
+                send(5 + kk, cd, kk, 4, l - 1, rep_of(h, y, cd), down_cond)
+            settle(four, right_send.at[k, 3 + kk], up_cond)
+            settle(four, right_send.at[k, 5 + kk], down_cond)
         remote(
             left.at[k, y, pl.ds(2 * other, 2)], right.at[k, 2, c],
-            right_send.at[k, 16], right_recv.at[k, 2, c, 0], l, rep_of(h, y, other),
+            right_send.at[k, 7], right_recv.at[k, 2, 0], l, rep_of(h, y, other),
         )
+        settle(four, right_send.at[k, 7])
         right[k, 2, c] = left[k, y, pl.ds(2 * c, 2)]
 
+    def got_chunk(k, n, kk, cond=None):
+        arrive(right.at[k, n, pl.ds(0, 2), kk], right_recv.at[k, n, kk], cond)
+
     def right_relay(k, parts=(0, 1, 2)):
-        def hand(at, n_from, n_to, cc, kk, layer, rep, cond):
-            remote(
-                right.at[k, n_from, cc, kk], right.at[k, n_to, cc, kk], right_send.at[k, at],
-                right_recv.at[k, n_to, cc, kk], layer, rep, cond,
-            )
-
-        def got_chunk(n, cc, kk, cond=None):
-            arrive(right.at[k, n, cc, kk], right_recv.at[k, n, cc, kk], cond)
-
-        def carried(which, kk, n, cond):
+        four, eight = left.at[k, y, pl.ds(0, 2)], left.at[k, y]
+        near = both(cross, delta != 2)
+        step = jnp.where(first, 3, 1)
+        want = mod(delta + step, 4) != jnp.where(first, 1, 3)
+
+        def hand(at, n_from, n_to, kk, layer, rep, cond):
             for cc in range(2):
-                arrive(stage.at[k, which, cc], stage_recv.at[k, which, cc], cond)
                 remote(
-                    stage.at[k, which, cc], right.at[k, n, cc, kk],
-                    right_send.at[k, 33 + 2 * which + cc], right_recv.at[k, n, cc, kk],
-                    l + 4 * over, rep_of(1 - h, y, c), cond,
+                    right.at[k, n_from, cc, kk], right.at[k, n_to, cc, kk], right_send.at[k, at],
+                    right_recv.at[k, n_to, kk], layer, rep, cond,
                 )
 
-        def pass_on(kk):
-            step = jnp.where(first, 3, 1)
-            want = mod(delta + step, 4) != jnp.where(first, 1, 3)
+        if 0 in parts:
+            got_chunk(k, 3 - 2 * h, 0)
+            hand(8, 3 - 2 * h, 1 + 2 * h, 0, ahead, rep_of(h, y, c), flat)
+            settle(four, right_send.at[k, 8], flat)
+            hand(11, 3 - 2 * h, 4 - 4 * h, 0, l + over, rep_of(1 - h, y, c), near)
+            got_chunk(k, 1 + 2 * h, 0, cross)
+            hand(10, 1 + 2 * h, 4 * h, 0, l, rep_of(1 - h, y, c), both(cross, want))
+            settle(four, right_send.at[k, 10], both(cross, want))
+        if 1 in parts:
+            arrive(stage.at[k], stage_recv.at[k], carry)
             for cc in range(2):
-                got_chunk(1 + 2 * h, cc, kk, cross)
-                hand(
-                    21 + 2 * kk + cc, 1 + 2 * h, 4 * h, cc, kk, l, rep_of(1 - h, y, c),
-                    both(cross, want),
+                remote(
+                    stage.at[k, cc], right.at[k, 3 - 2 * h, cc, 1], right_send.at[k, 12],
+                    right_recv.at[k, 3 - 2 * h, 1], l + 4 * over, rep_of(1 - h, y, c), carry,
                 )
-
-        near = both(cross, delta != 2)
-        if 0 in parts:
-            for cc in range(2):
-                got_chunk(3 - 2 * h, cc, 0)
-                hand(17 + cc, 3 - 2 * h, 1 + 2 * h, cc, 0, ahead, rep_of(h, y, c), flat)
-                hand(29 + cc, 3 - 2 * h, 4 - 4 * h, cc, 0, l + over, rep_of(1 - h, y, c), near)
-            pass_on(0)
-        if 1 in parts:
-            carried(0, 1, 3 - 2 * h, carry)
-            for cc in range(2):
-                got_chunk(4 - 4 * h, cc, 1, flat)
-                hand(19 + cc, 4 - 4 * h, 3 - 2 * h, cc, 1, l, rep_of(1 - h, y, c), flat)
+            settle(four, right_send.at[k, 12], carry)
+            got_chunk(k, 4 - 4 * h, 1, flat)
+            hand(9, 4 - 4 * h, 3 - 2 * h, 1, l, rep_of(1 - h, y, c), flat)
+            settle(four, right_send.at[k, 9], flat)
         if 2 in parts:
-            for cc in range(2):
-                got_chunk(3 - 2 * h, cc, 1, cross)
-                hand(31 + cc, 3 - 2 * h, 4 - 4 * h, cc, 1, l + over, rep_of(1 - h, y, c), near)
+            got_chunk(k, 3 - 2 * h, 1, cross)
+            hand(11, 3 - 2 * h, 4 - 4 * h, 1, l + over, rep_of(1 - h, y, c), near)
+            settle(eight, right_send.at[k, 11], near)
 
     def right_ready(k):
-        def got_chunk(n, cc, kk, cond=None):
-            arrive(right.at[k, n, cc, kk], right_recv.at[k, n, cc, kk], cond)
-
-        arrive(right.at[k, 2, other], right_recv.at[k, 2, other, 0])
+        arrive(right.at[k, 2, other], right_recv.at[k, 2, 0])
         low = both(below, delta != 1)
         high = both(above, delta != 3)
-        for cc in range(2):
-            got_chunk(3 - 2 * h, cc, 1, no(cross))
-            got_chunk(1 + 2 * h, cc, 0, flat_behind)
-            got_chunk(1 + 2 * h, cc, 1, either(flat_behind, cross))
-            got_chunk(0, cc, 0, low)
-            got_chunk(0, cc, 1, both(low, no(both(last, no(edge_down)))))
-            got_chunk(4, cc, 0, high)
-            got_chunk(4, cc, 1, both(high, no(both(first, no(edge_up)))))
+        got_chunk(k, 3 - 2 * h, 1, no(cross))
+        got_chunk(k, 1 + 2 * h, 0, flat_behind)
+        got_chunk(k, 1 + 2 * h, 1, either(flat_behind, cross))
+        got_chunk(k, 0, 0, low)
+        got_chunk(k, 0, 1, both(low, no(both(last, no(edge_down)))))
+        got_chunk(k, 4, 0, high)
+        got_chunk(k, 4, 1, both(high, no(both(first, no(edge_up)))))
 
     nothing = jnp.zeros((t, t), BF)
     apart = delta == 2
@@ -357,6 +362,7 @@
         remote(
             give.at[k], got.at[k], pair_send.at[k], pair_recv.at[k], l, rep_of(h, y, other)
         )
+        settle(give.at[k], pair_send.at[k])
         part = columns(c)
         for a in range(4):
             for b2 in range(2):
@@ -380,25 +386,25 @@
                 slot = mod(4 * y + 2 * c + b2 + shift - (4 * h + a) + 32, 16)
                 here = slot == r
                 mine = pltpu.make_async_copy(
-                    done.at[k, a, b2], out_ref.at[4 * h + a, 0], self_sem.at[k, a, b2]
+                    done.at[k, a, b2], out_ref.at[4 * h + a, 0], self_sem.at[k]
                 )
                 pl.when(here)(mine.start)
-                kept_here.append((here, mine))
                 remote(
-                    done.at[k, a, b2], out_ref.at[4 * h + a, 0], out_send.at[k, a, b2],
-                    out_recv.at[k, 4 * h + a], l, slot, slot != r,
+                    done.at[k, a, b2], out_ref.at[4 * h + a, 0], out_send.at[k],
+                    out_recv.at[k], l, slot, slot != r,
                 )
-
-    def owner_ready(k, out_ref):
-        for ap in range(8):
-            jm = mod(shift + ap + r, 16)
-            source = rep_of(ap // 4, div(jm, 4), div(mod(jm, 4), 2))
-            arrive(out_ref.at[ap, 0], out_recv.at[k, ap], source != r)
+        moved(kept.at[k], out_send.at[k])
+        for n in (1, 2):
+            mine = pltpu.make_async_copy(
+                kept.at[k, pl.ds(0, n)], out_ref.at[pl.ds(0, n), 0], self_sem.at[k]
+            )
+            kept_here.append((staying == n, mine))
+
+    def owner_ready(k):
+        arrived(kept.at[k], out_recv.at[k])
 
     def marks_ready():
-        for a in range(4):
-            for b2 in range(2):
-                arrive(marks_home.at[a, b2], mark_recv.at[a, b2], from_other(a, b2))
+        arrived(marks, mark_recv)
 
     def finish_u():
         arrive(got.at[U], pair_recv.at[U])
@@ -413,7 +419,8 @@
 
     scatter(Y)
     scatter(Z)
-    right_start(Y, home_ready)
+    home_ready(Y)
+    right_start(Y)
     home_ready(Z)
     left_start(Z)
     right_relay(Y, (0,))
@@ -448,8 +455,8 @@
     multiply(Y)
     arrive(got.at[Y], pair_recv.at[Y])
     owner_send(Y, x_out)
-    owner_ready(Z, w_out)
-    owner_ready(Y, x_out)
+    owner_ready(Z)
+    owner_ready(Y)
     for cond, copy in kept_here:
         pl.when(cond)(copy.wait)
     for cond, copy in pending:
@@ -474,38 +481,39 @@
             in_specs=[
                 pl.BlockSpec(memory_space=pl.ANY),
                 pl.BlockSpec(memory_space=pl.ANY),
-                pl.BlockSpec(memory_space=pltpu.SMEM),
+                pl.BlockSpec(memory_space=pl.ANY),
             ],
             out_specs=[pl.BlockSpec(memory_space=pl.ANY)] * 2,
             scratch_shapes=[
+                pltpu.SMEM((8,), jnp.int32),
                 pltpu.VMEM((2, 8, t, t), BF),
                 pltpu.VMEM((2, 8, t, t), BF),
                 pltpu.VMEM((8, 8, 128), jnp.int32),
                 pltpu.VMEM((4, 2, 8, 128), jnp.int32),
                 pltpu.VMEM((3, 4, 4, 2, t, t), BF),
                 pltpu.VMEM((3, 5, 2, 2, 2, t, t), BF),
-                pltpu.VMEM((3, 2, 2, 2, t, t), BF),
+                pltpu.VMEM((3, 2, 2, t, t), BF),
                 pltpu.VMEM((2, 4 * t, 6 * t), BF),
                 pltpu.VMEM((2, 2, 6 * t, 2 * t), BF),
                 pltpu.VMEM((4, 2, t, t), F32),
                 pltpu.VMEM((3, 4, 2, t, t), BF),
                 pltpu.VMEM((3, 4, 2, t, t), BF),
                 pltpu.VMEM((2, 4, 2, t, t), BF),
+                dma((3,)),
                 dma((2,)),
-                dma((2, 8)),
-                dma((2, 4, 2)),
-                dma((8,)),
-                dma((4, 2)),
-                dma((3, 6)),
-                dma((3, 6)),
-                dma((3, 37)),
-                dma((3, 5, 2, 2)),
-                dma((3, 2, 2)),
+                dma((2,)),
+                dma,
+                dma,
+                dma((3,)),
+                dma((3, 3)),
+                dma((3, 13)),
+                dma((3, 5, 2)),
                 dma((3,)),
                 dma((3,)),
-                dma((2, 4, 2)),
-                dma((2, 8)),
-                dma((2, 4, 2)),
+                dma((3,)),
+                dma((2,)),
+                dma((2,)),
+                dma((2,)),
             ],
             compiler_params=pltpu.CompilerParams(
                 collective_id=0, has_side_effects=True, vmem_limit_bytes=67043328

time: 68.1 us -> 65.2 us (0.957)
  Pallas kernels: 64.9 us -> 62 us
    pallas_call x1, Pallas kernels: 64.9 us -> 62 us  [body(): pl.pallas_call(functools.partial(kernel, layers, t), out_shape=[jax.Shape...]
where the time goes in v6:
time: 65.2 us; the launch traced here: 65 us
  Pallas kernels  62 us (95%)
  local copies, waits for them, and re-layouts  2.42 us (4%)
    pallas_call x1, Pallas kernels, body(): pl.pallas_call(functools.partial(kernel, layers, t), out_shape=[jax.Shape...  62 us
    unnamed x4, local copies, waits for them, and re-layouts  2.42 us

profile of v6, /device:TPU:71, one launch (start us, length us, event | category | flops | bytes accessed | tf_op | source)
XLA Modules:
  0.0 65.0 jit_solution(4829278217140417369)
XLA Ops:
  0.6 62.0 %band_step.1 = (bf16[8,1,128,128]{3,2,1,0:T(8,128)(2,1)}, bf16[8,1,128,128]{3,2,1,0:T(8,128)(2,1)}) custom-call(bf16[8,1,128,128]{3,2,1,0:T(8,128)(2,1)} %z_hbm.1, bf16[8,1,128,128]{3,2,1,0:T(8,128)(2,1)} %y_hbm.1, s32[8]{0:T(128)} %bitcast.1), custom_call_target="tpu_custom_call" | custom-call | tf_op jit(solution)/shard_map/band_step/pallas_call | solution.py:475
  62.6 0.0 copy-start
  62.6 1.7 %copy.7 = bf16[8,1,128,128]{3,2,1,0:T(8,128)(2,1)} copy(bf16[8,1,128,128]{3,2,1,0:T(8,128)(2,1)} %get-tuple-element.4) | data formatting | bytes 524288
  64.3 0.0 copy-done
  64.3 0.7 %copy.8 = bf16[8,1,128,128]{3,2,1,0:T(8,128)(2,1)} copy(bf16[8,1,128,128]{3,2,1,0:T(8,128)(2,1)S(1)} %copy-done) | data formatting | bytes 524288
Async XLA Ops:
  62.6 1.7 %copy-start = (bf16[8,1,128,128]{3,2,1,0:T(8,128)(2,1)S(1)}, bf16[8,1,128,128]{3,2,1,0:T(8,128)(2,1)}, u32[]{:S(2)}) copy-start(bf16[8,1,128,128]{3,2,1,0:T(8,128)(2,1)} %get-tuple-element.5) | copy-start | bytes 786436

commit v7 on v6

--- a/solution.py
+++ b/solution.py
@@ -376,13 +376,18 @@
         return marks_home[a, b2][0:1, :] == 1
 
     def owner_send(k, out_ref):
+        def finish(a, b2):
+            done[k, a, b2] = jnp.where(
+                marked(a, b2), summed(k, a, b2), jnp.zeros((t, t), F32)
+            ).astype(BF)
+
+        finish(0, 0)
+        finish(0, 1)
         for a in range(4):
             for b2 in range(2):
-                done[k, a, b2] = jnp.where(
-                    marked(a, b2), summed(k, a, b2), jnp.zeros((t, t), F32)
-                ).astype(BF)
-        for a in range(4):
-            for b2 in range(2):
+                after = 2 * a + b2 + 2
+                if after < 8:
+                    finish(after // 2, after % 2)
                 slot = mod(4 * y + 2 * c + b2 + shift - (4 * h + a) + 32, 16)
                 here = slot == r
                 mine = pltpu.make_async_copy(

time: 65.2 us -> 65.2 us (level)
  no operation moved by 1% of the time
where the time goes in v7:
time: 65.2 us; the launch traced here: 65 us
  Pallas kernels  62 us (95%)
  local copies, waits for them, and re-layouts  2.42 us (4%)
    pallas_call x1, Pallas kernels, body(): pl.pallas_call(functools.partial(kernel, layers, t), out_shape=[jax.Shape...  62 us
    unnamed x4, local copies, waits for them, and re-layouts  2.42 us

profile of v7, /device:TPU:71, one launch (start us, length us, event | category | flops | bytes accessed | tf_op | source)
XLA Modules:
  0.0 65.0 jit_solution(4220844335360013807)
XLA Ops:
  0.6 62.0 %band_step.1 = (bf16[8,1,128,128]{3,2,1,0:T(8,128)(2,1)}, bf16[8,1,128,128]{3,2,1,0:T(8,128)(2,1)}) custom-call(bf16[8,1,128,128]{3,2,1,0:T(8,128)(2,1)} %z_hbm.1, bf16[8,1,128,128]{3,2,1,0:T(8,128)(2,1)} %y_hbm.1, s32[8]{0:T(128)} %bitcast.1), custom_call_target="tpu_custom_call" | custom-call | tf_op jit(solution)/shard_map/band_step/pallas_call | solution.py:480
  62.6 0.0 copy-start
  62.6 1.7 %copy.7 = bf16[8,1,128,128]{3,2,1,0:T(8,128)(2,1)} copy(bf16[8,1,128,128]{3,2,1,0:T(8,128)(2,1)} %get-tuple-element.4) | data formatting | bytes 524288
  64.3 0.0 copy-done
  64.3 0.7 %copy.8 = bf16[8,1,128,128]{3,2,1,0:T(8,128)(2,1)} copy(bf16[8,1,128,128]{3,2,1,0:T(8,128)(2,1)S(1)} %copy-done) | data formatting | bytes 524288
Async XLA Ops:
  62.6 1.7 %copy-start = (bf16[8,1,128,128]{3,2,1,0:T(8,128)(2,1)S(1)}, bf16[8,1,128,128]{3,2,1,0:T(8,128)(2,1)}, u32[]{:S(2)}) copy-start(bf16[8,1,128,128]{3,2,1,0:T(8,128)(2,1)} %get-tuple-element.5) | copy-start | bytes 786436
